TPU v7x, 32 devices: a whole 2x2x4 slice. The times are simulated.
32 devices in a mesh: dp: 4 (over z), tensor: 8 (over y, x, core).
Axes of the slice: x: 2, y: 2, z: 4, core: 2. Of those that a mesh axis runs over, the one named last changes fastest.
Arguments:
- residual: float32 [8192, 4096], P(('dp', 'tensor')), may hold values from -6 to 6
- cotangent: bfloat16 [8192, 4096], P(('dp', 'tensor')), may hold values from -6 to 6
- segments: int32 [8, 1024], P('dp'), may hold values from 0 to 7, never falling along the last dimension, each value on 1 to 800 neighbouring positions
- in_proj: bfloat16 [4096, 32, 384], P('dp', 'tensor'), as said below
- qv_bias: bfloat16 [32, 256], P('tensor', 'dp'), may hold values from -1.5 to 1.5
- out_proj: bfloat16 [4096, 4096], P('tensor', 'dp'), may hold values from -0.25 to 0.25
- up_proj: bfloat16 [4096, 16384], P('dp', 'tensor'), may hold values from -0.09375 to 0.09375
- up_bias: bfloat16 [16384], P(('tensor', 'dp')), may hold values from -3 to 3
- down_proj: bfloat16 [16384, 4096], P('tensor', 'dp'), may hold values from -0.046875 to 0.046875
- norm_params: bfloat16 [4, 4096], replicated, may hold values from 0.099609375 to 1.8984375
- out_biases: bfloat16 [2, 4096], replicated, may hold values from -3 to 3
- first_in_proj: float32 [4096, 32, 384], P('dp', 'tensor'), may hold values from -16 to 16
- first_qv_bias: float32 [32, 256], P('tensor', 'dp'), may hold values from -16 to 16
- first_out_proj: float32 [4096, 4096], P('tensor', 'dp'), may hold values from -16 to 16
- first_up_proj: float32 [4096, 16384], P('dp', 'tensor'), may hold values from -16 to 16
- first_up_bias: float32 [16384], P(('tensor', 'dp')), may hold values from -16 to 16
- first_down_proj: float32 [16384, 4096], P('tensor', 'dp'), may hold values from -16 to 16
- first_norm_params: float32 [4, 4096], replicated, may hold values from -16 to 16
- first_out_biases: float32 [2, 4096], replicated, may hold values from -16 to 16
- second_in_proj: float32 [4096, 32, 384], P('dp', 'tensor'), may hold values from 1 to 100
- second_qv_bias: float32 [32, 256], P('tensor', 'dp'), may hold values from 1 to 100
- second_out_proj: float32 [4096, 4096], P('tensor', 'dp'), may hold values from 1 to 100
- second_up_proj: float32 [4096, 16384], P('dp', 'tensor'), may hold values from 1 to 100
- second_up_bias: float32 [16384], P(('tensor', 'dp')), may hold values from 1 to 100
- second_down_proj: float32 [16384, 4096], P('tensor', 'dp'), may hold values from 1 to 100
- second_norm_params: float32 [4, 4096], replicated, may hold values from 1 to 100
- second_out_biases: float32 [2, 4096], replicated, may hold values from 1 to 100
Outputs:
- output: float32 [8192, 4096], P(('dp', 'tensor'))
- grad_residual: float32 [8192, 4096], P(('dp', 'tensor'))
- grad_in_proj: float32 [4096, 32, 384], P('dp', 'tensor')
- new_in_proj: float32 [4096, 32, 384], P('dp', 'tensor')
- new_first_in_proj: float32 [4096, 32, 384], P('dp', 'tensor')
- new_second_in_proj: float32 [4096, 32, 384], P('dp', 'tensor')
- grad_qv_bias: float32 [32, 256], P('tensor', 'dp')
- new_qv_bias: float32 [32, 256], P('tensor', 'dp')
- new_first_qv_bias: float32 [32, 256], P('tensor', 'dp')
- new_second_qv_bias: float32 [32, 256], P('tensor', 'dp')
- grad_out_proj: float32 [4096, 4096], P('tensor', 'dp')
- new_out_proj: float32 [4096, 4096], P('tensor', 'dp')
- new_first_out_proj: float32 [4096, 4096], P('tensor', 'dp')
- new_second_out_proj: float32 [4096, 4096], P('tensor', 'dp')
- grad_up_proj: float32 [4096, 16384], P('dp', 'tensor')
- new_up_proj: float32 [4096, 16384], P('dp', 'tensor')
- new_first_up_proj: float32 [4096, 16384], P('dp', 'tensor')
- new_second_up_proj: float32 [4096, 16384], P('dp', 'tensor')
- grad_up_bias: float32 [16384], P(('tensor', 'dp'))
- new_up_bias: float32 [16384], P(('tensor', 'dp'))
- new_first_up_bias: float32 [16384], P(('tensor', 'dp'))
- new_second_up_bias: float32 [16384], P(('tensor', 'dp'))
- grad_down_proj: float32 [16384, 4096], P('tensor', 'dp')
- new_down_proj: float32 [16384, 4096], P('tensor', 'dp')
- new_first_down_proj: float32 [16384, 4096], P('tensor', 'dp')
- new_second_down_proj: float32 [16384, 4096], P('tensor', 'dp')
- grad_norm_params: float32 [4, 4096], replicated
- new_norm_params: float32 [4, 4096], replicated
- new_first_norm_params: float32 [4, 4096], replicated
- new_second_norm_params: float32 [4, 4096], replicated
- grad_out_biases: float32 [2, 4096], replicated
- new_out_biases: float32 [2, 4096], replicated
- new_first_out_biases: float32 [2, 4096], replicated
- new_second_out_biases: float32 [2, 4096], replicated
Inputs may be any that keep to these rules, and one draw needn't show every extreme that they name: `segments`: segment numbers never fall along a sequence; every segment holds 1 to 800 tokens, and some segment exactly 800. `in_proj`: entries of magnitude at most 36 times the inverse root of 4096.
All inputs are finite; a program needn't handle non-finite values.
Results may differ from a plain program's by a relative error of at most 0.0095.
The roundings to bfloat16 on the way count: a program that leaves them out, or rounds other values in their place, can miss the bound.
Values may be sent and summed in bfloat16 or wider, within the bound.
A program may use at most 640 MiB of HBM per device.

v0:
```python
import math

import jax
import jax.numpy as jnp
from jax import lax
from jax.sharding import PartitionSpec as P

D = 4096
HD = 128
ROT = 32
SEQ_LEN = 1024
STEP = 8


NORM_EPS = 1e-05
BETA_FIRST = 0.9
BETA_SECOND = 0.95
ADAM_EPS = 1e-08
LEARN_RATE = 0.01
WEIGHT_DECAY = 0.1
NEG_LARGE = -1e30


def positions_of(segments):
    index_grid = lax.broadcasted_iota(jnp.int32, segments.shape, 1)
    previous = jnp.concatenate([segments[:, :1] - 1, segments[:, :-1]], axis=1)
    starts = jnp.where(segments != previous, index_grid, 0)
    return index_grid - lax.cummax(starts, axis=1)


def rotation_tables(positions):
    half_rot = ROT // 2
    inv_freq = 10000.0 ** (-(2.0 * jnp.arange(half_rot, dtype=jnp.float32)) / ROT)
    angles = positions.astype(jnp.float32)[:, None] * inv_freq[None, :]
    cosine = jnp.concatenate([jnp.cos(angles), jnp.cos(angles)], axis=-1)
    sine_rows = jnp.concatenate([jnp.sin(angles), jnp.sin(angles)], axis=-1)
    return (cosine, sine_rows)


def rotate(source, cosine, sine_rows):
    half_rot = ROT // 2
    rot_part = source[..., :ROT]
    turned = jnp.concatenate([-rot_part[..., half_rot:], rot_part[..., :half_rot]], axis=-1)
    moved = rot_part * cosine[:, None, :] + turned * sine_rows[:, None, :]
    return jnp.concatenate([moved, source[..., ROT:]], axis=-1)


def normalize(source):
    centred = source - jnp.mean(source, axis=-1, keepdims=True)
    inv_std = lax.rsqrt(jnp.mean(centred * centred, axis=-1, keepdims=True) + NORM_EPS)
    return (centred * inv_std, inv_std)


def gelu_slope(source):
    return 0.5 * (1.0 + lax.erf(source * (1.0 / math.sqrt(2.0)))) + source * jnp.exp(
        -0.5 * source * source
    ) * (1.0 / math.sqrt(2.0 * math.pi))


def dot_nt(left_op, right_op):
    return lax.dot_general(
        left_op, right_op, (((1,), (1,)), ((), ())), preferred_element_type=jnp.float32
    )


def dot_tn(left_op, right_op):
    return lax.dot_general(
        left_op, right_op, (((0,), (0,)), ((), ())), preferred_element_type=jnp.float32
    )


def allowed_pairs(seg_row):
    length = seg_row.shape[0]
    index_grid = lax.broadcasted_iota(jnp.int32, (length, length), 0)
    column_grid = lax.broadcasted_iota(jnp.int32, (length, length), 1)
    return (column_grid <= index_grid) & (seg_row[:, None] == seg_row[None, :])


def masked_scores(queries, key_rows, seg_row):
    scaling = 1.0 / math.sqrt(HD)
    scores = (
        jnp.einsum("qhd,khd->hqk", queries, key_rows, preferred_element_type=jnp.float32) * scaling
    )
    return jnp.where(allowed_pairs(seg_row)[None], scores, NEG_LARGE)


def attend(packed):
    queries, key_rows, value_rows, seg_row = packed
    scores = masked_scores(queries, key_rows, seg_row)
    row_max = jnp.max(scores, axis=-1, keepdims=True)
    log_total = row_max + jnp.log(jnp.sum(jnp.exp(scores - row_max), axis=-1, keepdims=True))
    attn_prob = jnp.exp(scores - log_total).astype(jnp.bfloat16)
    mixed = jnp.einsum("hqk,khd->qhd", attn_prob, value_rows, preferred_element_type=jnp.float32)
    return (mixed.astype(jnp.bfloat16), log_total[..., 0])


def attend_back(packed):
    queries, key_rows, value_rows, attended, grad_att, log_total, seg_row = packed
    scaling = 1.0 / math.sqrt(HD)
    scores = masked_scores(queries, key_rows, seg_row)
    prob_full = jnp.exp(scores - log_total[..., None])
    prob_round = prob_full.astype(jnp.bfloat16)
    grad_prob = jnp.einsum("qhd,khd->hqk", grad_att, value_rows, preferred_element_type=jnp.float32)
    delta = jnp.sum(grad_att.astype(jnp.float32) * attended.astype(jnp.float32), axis=-1).T
    grad_scores = (scaling * prob_full * (grad_prob - delta[:, :, None])).astype(jnp.bfloat16)
    grad_queries = jnp.einsum(
        "hqk,khd->qhd", grad_scores, key_rows, preferred_element_type=jnp.float32
    )
    grad_keys = jnp.einsum("hqk,qhd->khd", grad_scores, queries, preferred_element_type=jnp.float32)
    grad_values = jnp.einsum(
        "hqk,qhd->khd", prob_round, grad_att, preferred_element_type=jnp.float32
    )
    return (grad_queries, grad_keys, grad_values)


def adamw(weight, gradient, first_m, second_m, decay_rate):
    new_first = BETA_FIRST * first_m + (1.0 - BETA_FIRST) * gradient
    new_second = BETA_SECOND * second_m + (1.0 - BETA_SECOND) * gradient * gradient
    bias_one = 1.0 - BETA_FIRST**STEP
    bias_two = 1.0 - BETA_SECOND**STEP
    weight_f = weight.astype(jnp.float32)
    update = (
        new_first / bias_one / (jnp.sqrt(new_second / bias_two) + ADAM_EPS) + decay_rate * weight_f
    )
    return (gradient, weight_f - LEARN_RATE * update, new_first, new_second)


def shards(
    residual,
    cotangent,
    segments,
    in_proj,
    qv_bias,
    out_proj,
    up_proj,
    up_bias,
    down_proj,
    norm_params,
    out_biases,
    first_in_proj,
    first_qv_bias,
    first_out_proj,
    first_up_proj,
    first_up_bias,
    first_down_proj,
    first_norm_params,
    first_out_biases,
    second_in_proj,
    second_qv_bias,
    second_out_proj,
    second_up_proj,
    second_up_bias,
    second_down_proj,
    second_norm_params,
    second_out_biases,
):
    norm_f = norm_params.astype(jnp.float32)
    rows_local = residual.shape[0]
    group_rows = lax.all_gather(residual, "tensor", axis=0, tiled=True)
    group_normed, group_inv = normalize(group_rows)
    attn_rows = (group_normed * norm_f[0] + norm_f[1]).astype(jnp.bfloat16)
    mlp_rows = (group_normed * norm_f[2] + norm_f[3]).astype(jnp.bfloat16)
    row_start = lax.axis_index("tensor") * rows_local
    normed = lax.dynamic_slice_in_dim(group_normed, row_start, rows_local, 0)
    inv_std = lax.dynamic_slice_in_dim(group_inv, row_start, rows_local, 0)
    grad_rows = lax.all_gather(cotangent, "tensor", axis=0, tiled=True)
    full_in, full_qv, full_out, full_up, full_upb, full_down = (
        lax.all_gather(in_proj, "dp", axis=0, tiled=True),
        lax.all_gather(qv_bias, "dp", axis=1, tiled=True),
        lax.all_gather(out_proj, "dp", axis=1, tiled=True),
        lax.all_gather(up_proj, "dp", axis=0, tiled=True),
        lax.all_gather(up_bias, "dp", axis=0, tiled=True),
        lax.all_gather(down_proj, "dp", axis=1, tiled=True),
    )
    heads_local = full_in.shape[1]
    rows_all = attn_rows.shape[0]
    seqs_local = segments.shape[0]
    in_matrix = full_in.reshape(D, heads_local * 3 * HD)
    projected = jnp.dot(attn_rows, in_matrix, preferred_element_type=jnp.float32).reshape(
        rows_all, heads_local, 3 * HD
    )
    positions = positions_of(segments).reshape(rows_all)
    cosine, sine_rows = rotation_tables(positions)
    bias_qv = full_qv.astype(jnp.float32)
    queries = rotate(projected[:, :, :HD] + bias_qv[:, :HD], cosine, sine_rows).astype(jnp.bfloat16)
    key_rows = rotate(projected[:, :, HD : 2 * HD], cosine, sine_rows).astype(jnp.bfloat16)
    value_rows = (projected[:, :, 2 * HD :] + bias_qv[:, HD:]).astype(jnp.bfloat16)

    def by_sequence(source):
        return source.reshape(seqs_local, SEQ_LEN, heads_local, HD)

    seq_queries = by_sequence(queries)
    seq_keys = by_sequence(key_rows)
    seq_values = by_sequence(value_rows)
    attended, log_total = lax.map(attend, (seq_queries, seq_keys, seq_values, segments))
    flat_out = attended.reshape(rows_all, heads_local * HD)
    up_rows = jnp.dot(mlp_rows, full_up, preferred_element_type=jnp.float32) + full_upb.astype(
        jnp.float32
    )
    activated = jax.nn.gelu(up_rows, approximate=False).astype(jnp.bfloat16)
    branch = jnp.dot(flat_out, full_out, preferred_element_type=jnp.float32) + jnp.dot(
        activated, full_down, preferred_element_type=jnp.float32
    )
    local_branch = lax.psum_scatter(branch, "tensor", scatter_dimension=0, tiled=True)
    bias_out = out_biases.astype(jnp.float32)
    output = residual + local_branch + bias_out[0] + bias_out[1]
    back_in, back_out, back_up, back_down = (
        lax.all_gather(in_proj, "dp", axis=0, tiled=True),
        lax.all_gather(out_proj, "dp", axis=1, tiled=True),
        lax.all_gather(up_proj, "dp", axis=0, tiled=True),
        lax.all_gather(down_proj, "dp", axis=1, tiled=True),
    )
    grad_up = dot_nt(grad_rows, back_down) * gelu_slope(up_rows)
    grad_up_r = grad_up.astype(jnp.bfloat16)
    grad_upb = jnp.sum(grad_up, axis=0)
    grad_down = dot_tn(activated, grad_rows)
    grad_upw = dot_tn(mlp_rows, grad_up_r)
    grad_mlp_in = dot_nt(grad_up_r, back_up)
    grad_flat = dot_nt(grad_rows, back_out).astype(jnp.bfloat16)
    grad_outw = dot_tn(flat_out, grad_rows)
    grad_queries, grad_keys, grad_values = lax.map(
        attend_back,
        (seq_queries, seq_keys, seq_values, attended, by_sequence(grad_flat), log_total, segments),
    )
    grad_queries = rotate(grad_queries.reshape(rows_all, heads_local, HD), cosine, -sine_rows)
    grad_keys = rotate(grad_keys.reshape(rows_all, heads_local, HD), cosine, -sine_rows)
    grad_values = grad_values.reshape(rows_all, heads_local, HD)
    grad_qv = jnp.concatenate(
        [jnp.sum(grad_queries, axis=0), jnp.sum(grad_values, axis=0)], axis=-1
    )
    grad_projected = (
        jnp.concatenate([grad_queries, grad_keys, grad_values], axis=-1)
        .astype(jnp.bfloat16)
        .reshape(rows_all, heads_local * 3 * HD)
    )
    grad_inw = dot_tn(attn_rows, grad_projected).reshape(D, heads_local, 3 * HD)
    grad_attn_in = dot_nt(grad_projected, back_in.reshape(D, heads_local * 3 * HD))
    shard_in, shard_qv, shard_outw, shard_upw, shard_upb, shard_down = (
        lax.psum_scatter(grad_inw, "dp", scatter_dimension=0, tiled=True),
        lax.psum_scatter(grad_qv, "dp", scatter_dimension=1, tiled=True),
        lax.psum_scatter(grad_outw, "dp", scatter_dimension=1, tiled=True),
        lax.psum_scatter(grad_upw, "dp", scatter_dimension=0, tiled=True),
        lax.psum_scatter(grad_upb, "dp", scatter_dimension=0, tiled=True),
        lax.psum_scatter(grad_down, "dp", scatter_dimension=1, tiled=True),
    )
    grad_norms_local = jnp.stack(
        [
            jnp.sum(grad_attn_in * group_normed, axis=0),
            jnp.sum(grad_attn_in, axis=0),
            jnp.sum(grad_mlp_in * group_normed, axis=0),
            jnp.sum(grad_mlp_in, axis=0),
        ]
    )
    group_grad = grad_attn_in * norm_f[0] + grad_mlp_in * norm_f[2]
    grad_normed = lax.psum_scatter(group_grad, "tensor", scatter_dimension=0, tiled=True)
    cotangent_f = cotangent.astype(jnp.float32)
    column_sum = jnp.sum(cotangent_f, axis=0)
    grad_ob_local = jnp.stack([column_sum, column_sum])
    grad_norms, grad_ob = lax.psum((grad_norms_local, grad_ob_local), ("dp", "tensor"))
    grad_residual = cotangent_f + inv_std * (
        grad_normed
        - jnp.mean(grad_normed, axis=-1, keepdims=True)
        - normed * jnp.mean(grad_normed * normed, axis=-1, keepdims=True)
    )
    result_in = adamw(in_proj, shard_in, first_in_proj, second_in_proj, WEIGHT_DECAY)
    result_qv = adamw(qv_bias, shard_qv, first_qv_bias, second_qv_bias, 0.0)
    result_out = adamw(out_proj, shard_outw, first_out_proj, second_out_proj, WEIGHT_DECAY)
    result_up = adamw(up_proj, shard_upw, first_up_proj, second_up_proj, WEIGHT_DECAY)
    result_upb = adamw(up_bias, shard_upb, first_up_bias, second_up_bias, 0.0)
    result_down = adamw(down_proj, shard_down, first_down_proj, second_down_proj, WEIGHT_DECAY)
    result_norm = adamw(norm_params, grad_norms, first_norm_params, second_norm_params, 0.0)
    result_ob = adamw(out_biases, grad_ob, first_out_biases, second_out_biases, 0.0)
    return (
        output,
        grad_residual,
        result_in[0],
        result_in[1],
        result_in[2],
        result_in[3],
        result_qv[0],
        result_qv[1],
        result_qv[2],
        result_qv[3],
        result_out[0],
        result_out[1],
        result_out[2],
        result_out[3],
        result_up[0],
        result_up[1],
        result_up[2],
        result_up[3],
        result_upb[0],
        result_upb[1],
        result_upb[2],
        result_upb[3],
        result_down[0],
        result_down[1],
        result_down[2],
        result_down[3],
        result_norm[0],
        result_norm[1],
        result_norm[2],
        result_norm[3],
        result_ob[0],
        result_ob[1],
        result_ob[2],
        result_ob[3],
    )


def solution(mesh):
    in_specs = (
        P(("dp", "tensor"), None),
        P(("dp", "tensor"), None),
        P("dp", None),
        P("dp", "tensor", None),
        P("tensor", "dp"),
        P("tensor", "dp"),
        P("dp", "tensor"),
        P(("tensor", "dp")),
        P("tensor", "dp"),
        P(),
        P(),
        P("dp", "tensor", None),
        P("tensor", "dp"),
        P("tensor", "dp"),
        P("dp", "tensor"),
        P(("tensor", "dp")),
        P("tensor", "dp"),
        P(),
        P(),
        P("dp", "tensor", None),
        P("tensor", "dp"),
        P("tensor", "dp"),
        P("dp", "tensor"),
        P(("tensor", "dp")),
        P("tensor", "dp"),
        P(),
        P(),
    )
    out_specs = (
        P(("dp", "tensor"), None),
        P(("dp", "tensor"), None),
        P("dp", "tensor", None),
        P("dp", "tensor", None),
        P("dp", "tensor", None),
        P("dp", "tensor", None),
        P("tensor", "dp"),
        P("tensor", "dp"),
        P("tensor", "dp"),
        P("tensor", "dp"),
        P("tensor", "dp"),
        P("tensor", "dp"),
        P("tensor", "dp"),
        P("tensor", "dp"),
        P("dp", "tensor"),
        P("dp", "tensor"),
        P("dp", "tensor"),
        P("dp", "tensor"),
        P(("tensor", "dp")),
        P(("tensor", "dp")),
        P(("tensor", "dp")),
        P(("tensor", "dp")),
        P("tensor", "dp"),
        P("tensor", "dp"),
        P("tensor", "dp"),
        P("tensor", "dp"),
        P(),
        P(),
        P(),
        P(),
        P(),
        P(),
        P(),
        P(),
    )
    return jax.shard_map(shards, mesh=mesh, in_specs=in_specs, out_specs=out_specs, check_vma=False)
```

profile of v0, /device:TPU:0, one launch (start us, length us, event | category | flops | bytes accessed | tf_op | source)
XLA Modules:
  0.0 3528.1 jit_solution(1955894836239016712)
XLA Ops:
  29.2 19.6 all-gather.1
  50.7 181.7 %all-gather.11.cloned.1.call-done = bf16[4096,4,384]{2,0,1:T(8,128)(2,1)} async-done(((bf16[1024,4,384]{2,0,1:T(8,128)(2,1)}), bf16[4096,4,384]{2,0,1:T(8,128)(2,1)}) %all-gather.11.cloned.1.call-update) | async-done | bytes 12582928 | tf_op jit(solution)/shard_map/all_gather | solution.py:168
  232.4 16.5 copy.126
  248.9 64.0 %all-gather.13.cloned.1.call-done = bf16[512,4096]{1,0:T(8,128)(2,1)} async-done(((bf16[512,1024]{1,0:T(8,128)(2,1)}), bf16[512,4096]{1,0:T(8,128)(2,1)}) %all-gather.13.cloned.1.call-update) | async-done | bytes 4194320 | tf_op jit(solution)/shard_map/all_gather | solution.py:170
  313.0 90.1 %all-gather.19.cloned.1.call-done = bf16[2048,4096]{1,0:T(8,128)(2,1)} async-done(((bf16[256,4096]{1,0:T(8,128)(2,1)}), bf16[2048,4096]{1,0:T(8,128)(2,1)}) %all-gather.19.cloned.1.call-update) | async-done | bytes 16777232 | tf_op jit(solution)/shard_map/all_gather | solution.py:166
  418.8 146.8 %all-gather.9.cloned.1.call-done = f32[2048,4096]{1,0:T(8,128)} async-done(((f32[256,4096]{1,0:T(8,128)}), f32[2048,4096]{1,0:T(8,128)}) %all-gather.9.cloned.1.call-update) | async-done | bytes 33554448 | tf_op jit(solution)/shard_map/all_gather | solution.py:159
  613.2 36.0 %fusion.61 = f32[2048,4,384]{0,2,1:T(8,128)} fusion(bf16[4096,4,384]{0,2,1:T(8,128)(2,1)} %copy.126, f32[2048,4096]{1,0:T(8,128)} %subtract_multiply_fusion, f32[4096]{0:T(1024)S(1)} %bitcast.240, f32[4096]{0:T(1024)S(1)} %bitcast.237), kind=kOutput, calls=%fused_computation.96 | convolution fusion | flops 25794969600 | bytes 58753024 | tf_op jit(solution)/shard_map/dot_general | solution.py:179
  706.3 31.9 while.26
  738.2 248.7 %while.27 = (s32[]{:T(128)}, f32[2,1024,4,128]{1,0,3,2:T(2,128)}, f32[2,1024,4,128]{1,0,3,2:T(2,128)}, f32[2,1024,4,128]{1,3,2,0:T(8,128)}, bf16[2,1024,4,128]{3...) while((s32[]{:T(128)}, f32[2,1024,4,128]{1,0,3,2:T(2,128)}, ...), condition=%wide.region_11.12_spmd, body=%wide.region_9.11_spmd.sunk | while | flops 5420085248 | bytes 163691248 | solution.py:221
  770.4 36.6 %dynamic_update_slice.30 = f32[2,1024,4,128]{1,0,3,2:T(2,128)} dynamic-update-slice(f32[2,1024,4,128]{1,0,3,2:T(2,128)} %get-tuple-element.554, f32[1,1024,4,128]{1,0,3,2:T(1,128)S(1)} %copy.221, s32[]{:T(128)} %get-tuple-element.552, s32[]{:T(128)} %constant.77.clone.1..sunk, s32[]{:T(128)} %constant.77.clone.1..sunk, s32[]{:T(128)} %constant.77.clone.1..sunk) | dynamic-update-slice | bytes 4194308 | tf_op jit(solution)/shard_map/while/body/jit(dynamic_update_index_in_dim)/dynamic_update_slice | solution.py:221
  815.8 36.6 %dynamic_update_slice.29 = f32[2,1024,4,128]{1,0,3,2:T(2,128)} dynamic-update-slice(f32[2,1024,4,128]{1,0,3,2:T(2,128)} %get-tuple-element.553, f32[1,1024,4,128]{1,0,3,2:T(1,128)S(1)} %copy.220, s32[]{:T(128)} %get-tuple-element.552, s32[]{:T(128)} %constant.77.clone.1..sunk, s32[]{:T(128)} %constant.77.clone.1..sunk, s32[]{:T(128)} %constant.77.clone.1..sunk) | dynamic-update-slice | bytes 4194308 | tf_op jit(solution)/shard_map/while/body/jit(dynamic_update_index_in_dim)/dynamic_update_slice | solution.py:221
  894.9 36.6 %dynamic_update_slice.30 = f32[2,1024,4,128]{1,0,3,2:T(2,128)} dynamic-update-slice(f32[2,1024,4,128]{1,0,3,2:T(2,128)} %get-tuple-element.554, f32[1,1024,4,128]{1,0,3,2:T(1,128)S(1)} %copy.221, s32[]{:T(128)} %get-tuple-element.552, s32[]{:T(128)} %constant.77.clone.1..sunk, s32[]{:T(128)} %constant.77.clone.1..sunk, s32[]{:T(128)} %constant.77.clone.1..sunk) | dynamic-update-slice | bytes 4194308 | tf_op jit(solution)/shard_map/while/body/jit(dynamic_update_index_in_dim)/dynamic_update_slice | solution.py:221
  940.3 36.6 %dynamic_update_slice.29 = f32[2,1024,4,128]{1,0,3,2:T(2,128)} dynamic-update-slice(f32[2,1024,4,128]{1,0,3,2:T(2,128)} %get-tuple-element.553, f32[1,1024,4,128]{1,0,3,2:T(1,128)S(1)} %copy.220, s32[]{:T(128)} %get-tuple-element.552, s32[]{:T(128)} %constant.77.clone.1..sunk, s32[]{:T(128)} %constant.77.clone.1..sunk, s32[]{:T(128)} %constant.77.clone.1..sunk) | dynamic-update-slice | bytes 4194308 | tf_op jit(solution)/shard_map/while/body/jit(dynamic_update_index_in_dim)/dynamic_update_slice | solution.py:221
  1045.5 81.4 %fusion.47 = (bf16[2048,2048]{1,0:T(8,128)(2,1)}, f32[2048,2048]{1,0:T(8,128)}) fusion(f32[2048]{0:T(1024)S(1)} %bitcast.246, bf16[4096,2048]{1,0:T(8,128)(2,1)} %all-gather.15.cloned.1.call-done, f32[2048,4096]{1,0:T(8,128)} %subtract_multiply_fusion, f32[4096]{0:T(1024)S(1)} %bitcast.235, f32[4096]{0:T(1024)S(1)} %bitcast.232), kind=kOutput, calls=%fused_computation.74 | convolution fusion | flops 34661728256 | bytes 75538432 | tf_op jit(solution)/shard_map/dot_general | solution.py:197
  1140.1 52.5 %fusion.122 = (f32[2048]{0:T(1024)}, bf16[2048,2048]{1,0:T(8,128)(2,1)}) fusion(f32[2048,2048]{1,0:T(8,128)} %get-tuple-element.391, f32[2048]{0:T(1024)S(1)} %bitcast.247, bf16[2048,4096]{1,0:T(8,128)(2,1)} %all-gather.19.cloned.1.call-done, bf16[2048,4096]{1,0:T(8,128)(2,1)} %all-gather.17.cloned.1.call-done), kind=kOutput, calls=%fused_computation.220 | convolution fusion | flops 34410070016 | bytes 58736640 | tf_op jit(solution)/shard_map/dot_general | solution.py:61
  1192.6 44.0 %fusion.79 = f32[2048,4096]{1,0:T(8,128)} fusion(bf16[4096,2048]{1,0:T(8,128)(2,1)} %all-gather.15.cloned.1.call-done, bf16[2048,2048]{1,0:T(8,128)(2,1)} %get-tuple-element.393), kind=kOutput, calls=%fused_computation.133 | convolution fusion | flops 34359738368 | bytes 58720256 | tf_op jit(solution)/shard_map/dot_general | solution.py:61
  1236.6 45.9 %fusion.44 = (f32[4096]{0:T(1024)S(1)}, f32[4096]{0:T(1024)S(1)}, f32[4096]{0:T(1024)S(1)}, f32[4096]{0:T(1024)S(1)}, f32[2048,4096]{1,0:T(8,128)}) fusion(f32[2048,4096]{1,0:T(8,128)} %subtract_multiply_fusion, f32[2048,4096]{1,0:T(8,128)} %fusion.79, f32[4096]{0:T(1024)S(1)} %bitcast.233, f32[4096]{0:T(1024)S(1)} %bitcast.238, ...), kind=kOutput, calls=%fused_computation.63 | convolution fusion | flops 25845284864 | bytes 119635968 | tf_op jit(solution)/shard_map/dot_general | solution.py:61
  1285.8 15.6 fusion.84
  1310.1 34.7 fusion.72
  1346.6 16.7 fusion.86
  1363.3 46.0 %convolution_add_fusion = f32[2048,4096]{1,0:T(8,128)} fusion(f32[2048,4096]{1,0:T(8,128)} %fusion.86, bf16[2048,2048]{1,0:T(8,128)(2,1)} %get-tuple-element.390, bf16[2048,4096]{1,0:T(8,128)(2,1)} %all-gather.17.cloned.1.call-done), kind=kOutput, calls=%fused_computation.71 | convolution fusion | flops 34368126976 | bytes 92274688 | tf_op jit(solution)/shard_map/dot_general | solution.py:201
  1410.0 44.0 %fusion.75 = f32[4096,2048]{1,0:T(8,128)} fusion(f32[2048,4096]{1,0:T(8,128)} %subtract_multiply_fusion, f32[4096]{0:T(1024)S(1)} %bitcast.236, f32[4096]{0:T(1024)S(1)} %bitcast.234, bf16[2048,2048]{1,0:T(8,128)(2,1)} %get-tuple-element.393), kind=kOutput, calls=%fused_computation.125 | convolution fusion | flops 34384904192 | bytes 75530240 | tf_op jit(solution)/shard_map/dot_general | solution.py:67
  1454.0 44.2 %fusion.123 = f32[2048,4096]{1,0:T(8,128)} fusion(bf16[2048,2048]{1,0:T(8,128)(2,1)} %get-tuple-element.390, bf16[2048,4096]{1,0:T(8,128)(2,1)} %all-gather.19.cloned.1.call-done), kind=kOutput, calls=%fused_computation.221 | convolution fusion | flops 34359738368 | bytes 58720256 | tf_op jit(solution)/shard_map/dot_general | solution.py:67
  1514.1 39.3 %reduce-scatter.16.cloned.1.call-done = f32[512,1024]{1,0:T(8,128)} async-done(((f32[512,4096]{1,0:T(8,128)}), f32[512,1024]{1,0:T(8,128)}) %reduce-scatter.16.cloned.1.call-update) | async-done | bytes 2097168 | tf_op jit(solution)/shard_map/reduce_scatter | solution.py:241
  1559.7 410.6 %reduce-scatter.14.cloned.1.call-done = f32[1024,4,384]{2,0,1:T(8,128)} async-done(((f32[4096,4,384]{2,0,1:T(8,128)}), f32[1024,4,384]{2,0,1:T(8,128)}) %reduce-scatter.14.cloned.1.call-update) | async-done | bytes 6291472 | tf_op jit(solution)/shard_map/reduce_scatter | solution.py:239
  2015.7 165.8 %reduce-scatter.12.cloned.1.call-done = f32[256,4096]{1,0:T(8,128)} async-done(((f32[2048,4096]{1,0:T(8,128)}), f32[256,4096]{1,0:T(8,128)}) %reduce-scatter.12.cloned.1.call-update) | async-done | bytes 4194320 | tf_op jit(solution)/shard_map/reduce_scatter | solution.py:255
  2192.0 39.8 %psum.15 = f32[2,4096]{1,0:T(2,128)S(1)} all-reduce(f32[2,4096]{1,0:T(2,128)S(1)} %pad_maximum_fusion.5), channel_id=1, replica_groups=mesh['dp'=4,'tensor'=8] {'dp','tensor'}, use_global_device_ids=true, to_apply=%region_30.31 | all-reduce | flops 8192 | bytes 65536 | tf_op jit(solution)/shard_map/psum | solution.py:259
  2232.6 157.9 %reduce-scatter.10.cloned.1.call-done = f32[256,4096]{1,0:T(8,128)} async-done(((f32[2048,4096]{1,0:T(8,128)}), f32[256,4096]{1,0:T(8,128)}) %reduce-scatter.10.cloned.1.call-update) | async-done | bytes 4194320 | tf_op jit(solution)/shard_map/reduce_scatter | solution.py:204
  2396.9 548.7 %reduce-scatter.18.cloned.1.call-done = f32[1024,2048]{1,0:T(8,128)} async-done(((f32[4096,2048]{1,0:T(8,128)}), f32[1024,2048]{1,0:T(8,128)}) %reduce-scatter.18.cloned.1.call-update) | async-done | bytes 8388624 | tf_op jit(solution)/shard_map/reduce_scatter | solution.py:242
  2945.6 20.7 convert_subtract_fusion.1
  2966.4 534.9 %reduce-scatter.20.cloned.1.call-done = f32[2048,1024]{1,0:T(8,128)} async-done(((f32[2048,4096]{1,0:T(8,128)}), f32[2048,1024]{1,0:T(8,128)}) %reduce-scatter.20.cloned.1.call-update) | async-done | bytes 8388624 | tf_op jit(solution)/shard_map/reduce_scatter | solution.py:244
  3501.2 19.3 convert_subtract_fusion
  (274 shorter events, 448.7 us)
Async XLA Ops:
  7.2 225.2 %all-gather.11.cloned.1.call-start = ((), (), s32[]{:S(2)}) async-start(), calls=%async_computation.8 | async-start | bytes 15728640 | tf_op jit(solution)/shard_map/all_gather | solution.py:168
  11.3 16.8 copy-start.15
  11.3 17.9 copy-start.40
  11.3 301.7 %all-gather.13.cloned.1.call-start = ((), (), s32[]{:S(2)}) async-start(), calls=%async_computation.9 | async-start | bytes 5242880 | tf_op jit(solution)/shard_map/all_gather | solution.py:170
  12.0 391.1 %all-gather.19.cloned.1.call-start = ((), (), s32[]{:S(2)}) async-start(), calls=%async_computation.13 | async-start | bytes 18874368 | tf_op jit(solution)/shard_map/all_gather | solution.py:166
  12.8 552.8 %all-gather.9.cloned.1.call-start = ((), (), s32[]{:S(2)}) async-start(), calls=%async_computation.7 | async-start | bytes 37748736 | tf_op jit(solution)/shard_map/all_gather | solution.py:159
  13.4 1032.1 %all-gather.15.cloned.1.call-start = ((), (), s32[]{:S(2)}) async-start(), calls=%async_computation.10 | async-start | bytes 20971520 | tf_op jit(solution)/shard_map/all_gather | solution.py:171
  13.9 1126.2 %all-gather.17.cloned.1.call-start = ((), (), s32[]{:S(2)}) async-start(), calls=%async_computation.11 | async-start | bytes 20971520 | tf_op jit(solution)/shard_map/all_gather | solution.py:173
  14.5 1496.5 %reduce-scatter.22.cloned.1.call-start = ((), (), s32[]{:S(2)}) async-start(), calls=%async_computation.20 | async-start | bytes 163840
  15.3 597.8 %copy-start.33 = (f32[1,4096]{1,0:T(1,128)}, f32[1,4096]{1,0:T(1,128)S(1)}, u32[]{:S(2)}) copy-start(f32[1,4096]{1,0:T(1,128)S(1)} %get-tuple-element.382) | copy-start | bytes 49156
  15.3 597.8 %copy-start.35 = (f32[1,4096]{1,0:T(1,128)}, f32[1,4096]{1,0:T(1,128)S(1)}, u32[]{:S(2)}) copy-start(f32[1,4096]{1,0:T(1,128)S(1)} %get-tuple-element.383) | copy-start | bytes 49156
  50.7 608.6 %copy-start.9 = (f32[2048,32]{0,1:T(8,128)}, f32[2048,32]{0,1:T(8,128)S(1)}, u32[]{:S(2)}) copy-start(f32[2048,32]{0,1:T(8,128)S(1)} %get-tuple-element.394) | copy-start | bytes 786436
  578.8 22.2 copy-start.1
  1032.1 480.3 %all-reduce.3.cloned.1.call-start = ((), (), s32[]{:S(2)}) async-start(), calls=%async_computation.19 | async-start | bytes 131072 | tf_op jit(solution)/shard_map/psum | solution.py:259
  1192.6 44.0 %copy-start.5 = (bf16[2048,4,384]{2,0,1:T(8,128)(2,1)S(1)}, bf16[2048,4,384]{2,0,1:T(8,128)(2,1)}, u32[]{:S(2)}) copy-start(bf16[2048,4,384]{2,0,1:T(8,128)(2,1)} %concatenate.66) | copy-start | bytes 18874372
  1192.6 44.0 %copy-start.29 = (f32[1,4096]{1,0:T(1,128)S(1)}, f32[1,4096]{1,0:T(1,128)}, u32[]{:S(2)}) copy-start(f32[1,4096]{1,0:T(1,128)} %get-tuple-element.380) | copy-start | bytes 49156
  1192.6 44.0 %copy-start.34 = (f32[1,4096]{1,0:T(1,128)S(1)}, f32[1,4096]{1,0:T(1,128)}, u32[]{:S(2)}) copy-start(f32[1,4096]{1,0:T(1,128)} %copy-done.33) | copy-start | bytes 49156
  1236.6 46.7 %copy-start.4 = (bf16[2,1024,4,128]{1,3,2,0:T(8,128)(2,1)S(1)}, bf16[2,1024,4,128]{1,3,2,0:T(8,128)(2,1)}, u32[]{:S(2)}) copy-start(bf16[2,1024,4,128]{1,3,2,0:T(8,128)(2,1)} %get-tuple-element.637) | copy-start | bytes 6291460
  1285.8 267.6 %reduce-scatter.16.cloned.1.call-start = ((), (), s32[]{:S(2)}) async-start(), calls=%async_computation.16 | async-start | bytes 10485760 | tf_op jit(solution)/shard_map/reduce_scatter | solution.py:241
  1301.5 668.9 %reduce-scatter.14.cloned.1.call-start = ((), (), s32[]{:S(2)}) async-start(), calls=%async_computation.15 | async-start | bytes 31457280 | tf_op jit(solution)/shard_map/reduce_scatter | solution.py:239
  1344.9 836.6 %reduce-scatter.12.cloned.1.call-start = ((), (), s32[]{:S(2)}) async-start(), calls=%async_computation.14 | async-start | bytes 37748736 | tf_op jit(solution)/shard_map/reduce_scatter | solution.py:255
  1345.6 1044.8 %reduce-scatter.10.cloned.1.call-start = ((), (), s32[]{:S(2)}) async-start(), calls=%async_computation.12 | async-start | bytes 37748736 | tf_op jit(solution)/shard_map/reduce_scatter | solution.py:204
  1409.3 1536.3 %reduce-scatter.18.cloned.1.call-start = ((), (), s32[]{:S(2)}) async-start(), calls=%async_computation.17 | async-start | bytes 41943040 | tf_op jit(solution)/shard_map/reduce_scatter | solution.py:242
  1454.0 2047.3 %reduce-scatter.20.cloned.1.call-start = ((), (), s32[]{:S(2)}) async-start(), calls=%async_computation.18 | async-start | bytes 41943040 | tf_op jit(solution)/shard_map/reduce_scatter | solution.py:244
  1498.3 55.1 %copy-start.11 = (bf16[512,1024]{1,0:T(8,128)(2,1)S(1)}, bf16[512,1024]{1,0:T(8,128)(2,1)}, u32[]{:S(2)}) copy-start(bf16[512,1024]{1,0:T(8,128)(2,1)} %param.36) | copy-start | bytes 3145732
  1498.3 55.1 %copy-start.14 = (f32[512,1024]{1,0:T(8,128)S(1)}, f32[512,1024]{1,0:T(8,128)}, u32[]{:S(2)}) copy-start(f32[512,1024]{1,0:T(8,128)} %param.44) | copy-start | bytes 6291460
  1511.8 470.4 %copy-start.39 = (f32[4,64]{1,0:T(4,128)}, f32[4,64]{1,0:T(4,128)S(1)}, u32[]{:S(2)}) copy-start(f32[4,64]{1,0:T(4,128)S(1)} %copy.160) | copy-start | bytes 3076
  2008.2 177.8 %copy-start.8 = (bf16[256,4096]{1,0:T(8,128)(2,1)S(1)}, bf16[256,4096]{1,0:T(8,128)(2,1)}, u32[]{:S(2)}) copy-start(bf16[256,4096]{1,0:T(8,128)(2,1)} %param.32) | copy-start | bytes 6291460
  2185.9 45.8 %copy-start.26 = (f32[2,4096]{1,0:T(2,128)S(1)}, f32[2,4096]{1,0:T(2,128)}, u32[]{:S(2)}) copy-start(f32[2,4096]{1,0:T(2,128)} %param.49) | copy-start | bytes 98308
  2186.0 45.8 %copy-start.27 = (f32[2,4096]{1,0:T(2,128)S(1)}, f32[2,4096]{1,0:T(2,128)}, u32[]{:S(2)}) copy-start(f32[2,4096]{1,0:T(2,128)} %param.57) | copy-start | bytes 98308
  2231.8 734.6 %copy-start.22 = (f32[2,4096]{1,0:T(2,128)}, f32[2,4096]{1,0:T(2,128)S(1)}, u32[]{:S(2)}) copy-start(f32[2,4096]{1,0:T(2,128)S(1)} %psum.15) | copy-start | bytes 98308
  2966.3 554.2 %copy-start.19 = (f32[4,4096]{1,0:T(4,128)S(1)}, f32[4,4096]{1,0:T(4,128)}, u32[]{:S(2)}) copy-start(f32[4,4096]{1,0:T(4,128)} %all-reduce.3.cloned.1.call-done) | copy-start | bytes 196612
  (36 other events, 341.5 us)
Sparse Core Ops, SparseCore 0:
  11.4 221.0 all-gather.10
  234.0 78.9 all-gather.12
  314.9 88.2 all-gather.18
  404.8 160.6 all-gather.8
  567.0 286.7 all-gather.14
  855.2 284.9 all-gather.16
  1142.9 17.6 reduce-scatter.21
  1285.9 117.5 all-reduce.2
  1407.0 146.3 reduce-scatter.15
  1555.6 414.7 reduce-scatter.13
  1974.0 207.4 reduce-scatter.11
  2184.9 205.4 reduce-scatter.9
  2393.4 552.1 reduce-scatter.17
  2948.4 552.8 reduce-scatter.19
where the time goes:
time: 3550 us; the launch traced here: 3530 us
  waiting for transfers between devices  2360 us (66%)
  matrix products  574 us (16%)
  local copies, waits for them, and re-layouts  338 us (10%)
  other arithmetic  161 us (5%)
  blocking collectives  81.4 us (2%)
    reduce_scatter x1, waiting for transfers between devices, shards(): lax.psum_scatter(grad_upw, 'dp', scatter_dimension=0, tiled=True)  549 us
    reduce_scatter x1, waiting for transfers between devices, shards(): lax.psum_scatter(grad_down, 'dp', scatter_dimension=1, tiled=True)  535 us
    reduce_scatter x1, waiting for transfers between devices, shards(): lax.psum_scatter(grad_inw, 'dp', scatter_dimension=0, tiled=True)  411 us
    all_gather x1, waiting for transfers between devices, shards(): lax.all_gather(in_proj, 'dp', axis=0, tiled=True)  182 us
    reduce_scatter x1, waiting for transfers between devices, shards(): lax.psum_scatter(group_grad, 'tensor', scatter_dimension=0, tiled=True)  166 us
    reduce_scatter x1, waiting for transfers between devices, shards(): lax.psum_scatter(branch, 'tensor', scatter_dimension=0, tiled=True)  158 us
    dot_general x4, matrix products, dot_nt(): lax.dot_general(left_op, right_op, (((1,), (1,)), ((), ())), preferred_el...  156 us
    dynamic_update_slice x8, local copies, waits for them, and re-layouts, shards(): lax.map(attend_back, (seq_queries, seq_keys, seq_values, attended, by_seq...  155 us
  transfers between devices with their start and end apart: 14, of which 11 were waited for; matrix products, arithmetic and copies ran while one was open for 29% of the time, Pallas kernels for 0%

commit v1 on v0

v1 whole, which is shorter than its diff:
```python
import functools
import math

import jax
import jax.numpy as jnp
from jax import lax
from jax.experimental import pallas as pl
from jax.experimental.pallas import tpu as pltpu
from jax.sharding import PartitionSpec as P


D = 4096
HD = 128
ROT = 32
SEQ_LEN = 1024
STEP = 8
DOCS = 8

NORM_EPS = 1e-05
BETA_FIRST = 0.9
BETA_SECOND = 0.95
ADAM_EPS = 1e-08
LEARN_RATE = 0.01
WEIGHT_DECAY = 0.1
NEG_LARGE = -1e30
Q_BLOCK = 256
PACK = 16

F32 = jnp.float32
BF16 = jnp.bfloat16


def positions_of(segments):
    numbers = jnp.arange(DOCS, dtype=jnp.int32)
    below = segments[:, None, :] < numbers[None, :, None]
    starts = jnp.sum(below.astype(jnp.int32), axis=-1)
    own = segments[:, :, None] == numbers[None, None, :]
    start = jnp.sum(jnp.where(own, starts[:, None, :], 0), axis=-1)
    return lax.broadcasted_iota(jnp.int32, segments.shape, 1) - start


def rotation_tables(positions):
    half_rot = ROT // 2
    inv_freq = 10000.0 ** (-(2.0 * jnp.arange(half_rot, dtype=F32)) / ROT)
    angles = positions.astype(F32)[:, None] * inv_freq[None, :]
    cosine, sine = jnp.cos(angles), jnp.sin(angles)
    rows = positions.shape[0]
    rest = HD - ROT
    ones, zeros = jnp.ones((rows, rest), F32), jnp.zeros((rows, rest), F32)
    half = jnp.zeros_like(sine)
    return (
        jnp.concatenate([cosine, cosine, ones], axis=-1),
        jnp.concatenate([-sine, half, zeros], axis=-1),
        jnp.concatenate([half, sine, zeros], axis=-1),
    )


def normalize(source):
    centred = source - jnp.mean(source, axis=-1, keepdims=True)
    inv_std = lax.rsqrt(jnp.mean(centred * centred, axis=-1, keepdims=True) + NORM_EPS)
    return centred * inv_std, inv_std


def dot_nt(left_op, right_op):
    return lax.dot_general(left_op, right_op, (((1,), (1,)), ((), ())), preferred_element_type=F32)


def dot_tn(left_op, right_op):
    return lax.dot_general(left_op, right_op, (((0,), (0,)), ((), ())), preferred_element_type=F32)


def attention_kernel(
    proj_ref, bias_ref, cos_ref, right_ref, left_ref, seg_col_ref, seg_row_ref, grad_ref,
    attended_ref, gproj_ref, gqv_ref, key_sum, value_sum,
):
    scaling = 1.0 / math.sqrt(HD)
    cosine, from_right, from_left = cos_ref[...], right_ref[...], left_ref[...]
    half_rot = ROT // 2

    def turn(source, sign):
        return source * cosine + sign * (
            pltpu.roll(source, HD - half_rot, 1) * from_right
            + pltpu.roll(source, half_rot, 1) * from_left
        )

    bias = bias_ref[0]
    queries = turn(proj_ref[:, :HD] + bias[:, :HD], 1.0).astype(BF16)
    keys = turn(proj_ref[:, HD : 2 * HD], 1.0).astype(BF16)
    values = (proj_ref[:, 2 * HD :] + bias[:, HD:]).astype(BF16)
    key_sum[...] = jnp.zeros_like(key_sum)
    value_sum[...] = jnp.zeros_like(value_sum)
    query_parts = []
    for start in range(0, SEQ_LEN, Q_BLOCK):
        rows = slice(start, start + Q_BLOCK)
        reach = start + Q_BLOCK
        query, grad = queries[rows], grad_ref[rows, :]
        key, value = keys[:reach], values[:reach]
        scores = dot_nt(query, key) * scaling
        row_at = lax.broadcasted_iota(jnp.int32, (Q_BLOCK, reach), 0) + start
        column_at = lax.broadcasted_iota(jnp.int32, (Q_BLOCK, reach), 1)
        allowed = (column_at <= row_at) & (seg_col_ref[0, rows, :] == seg_row_ref[0, :, :reach])
        scores = jnp.where(allowed, scores, NEG_LARGE)
        weights = jnp.exp(scores - jnp.max(scores, axis=-1, keepdims=True))
        prob = weights * (1.0 / jnp.sum(weights, axis=-1, keepdims=True))
        prob_round = prob.astype(BF16)
        mixed = jnp.dot(prob_round, value, preferred_element_type=F32).astype(BF16)
        attended_ref[rows, :] = mixed
        delta = jnp.sum(grad.astype(F32) * mixed.astype(F32), axis=-1, keepdims=True)
        grad_prob = dot_nt(grad, value)
        grad_scores = (scaling * prob * (grad_prob - delta)).astype(BF16)
        query_parts.append(jnp.dot(grad_scores, key, preferred_element_type=F32))
        key_sum[:reach, :] += dot_tn(grad_scores, query)
        value_sum[:reach, :] += dot_tn(prob_round, grad)
    grad_query = turn(jnp.concatenate(query_parts, axis=0), -1.0)
    grad_value = value_sum[...]
    gproj_ref[:, :HD] = grad_query.astype(BF16)
    gproj_ref[:, HD : 2 * HD] = turn(key_sum[...], -1.0).astype(BF16)
    gproj_ref[:, 2 * HD :] = grad_value.astype(BF16)
    gqv_ref[0, 0, :, :HD] = jnp.sum(grad_query, axis=0, keepdims=True)
    gqv_ref[0, 0, :, HD:] = jnp.sum(grad_value, axis=0, keepdims=True)


def attention(projected, bias_qv, tables, segments, grad_flat):
    seqs, heads = segments.shape[0], bias_qv.shape[0]
    rows = seqs * SEQ_LEN
    table = pl.BlockSpec((SEQ_LEN, HD), lambda s, h: (s, 0))
    head = pl.BlockSpec((SEQ_LEN, HD), lambda s, h: (s, h))
    packed = pl.BlockSpec((SEQ_LEN, 3 * HD), lambda s, h: (s, h))
    pairs = seqs * heads * SEQ_LEN * SEQ_LEN
    return pl.pallas_call(
        attention_kernel,
        grid=(seqs, heads),
        in_specs=[
            packed,
            pl.BlockSpec((1, 1, 2 * HD), lambda s, h: (h, 0, 0)),
            table,
            table,
            table,
            pl.BlockSpec((1, SEQ_LEN, 1), lambda s, h: (s, 0, 0)),
            pl.BlockSpec((1, 1, SEQ_LEN), lambda s, h: (s, 0, 0)),
            head,
        ],
        out_specs=[head, packed, pl.BlockSpec((1, 1, 1, 2 * HD), lambda s, h: (s, h, 0, 0))],
        out_shape=[
            jax.ShapeDtypeStruct((rows, heads * HD), BF16),
            jax.ShapeDtypeStruct((rows, heads * 3 * HD), BF16),
            jax.ShapeDtypeStruct((seqs, heads, 1, 2 * HD), F32),
        ],
        scratch_shapes=[pltpu.VMEM((SEQ_LEN, HD), F32), pltpu.VMEM((SEQ_LEN, HD), F32)],
        cost_estimate=pl.CostEstimate(
            flops=12 * pairs * HD, bytes_accessed=rows * heads * HD * 24, transcendentals=pairs
        ),
        name="attention",
    )(
        projected,
        bias_qv[:, None, :],
        *tables,
        segments[:, :, None],
        segments[:, None, :],
        grad_flat,
    )


def adamw(weight, gradient, first_m, second_m, decay_rate):
    new_first = BETA_FIRST * first_m + (1.0 - BETA_FIRST) * gradient
    new_second = BETA_SECOND * second_m + (1.0 - BETA_SECOND) * gradient * gradient
    bias_one = 1.0 - BETA_FIRST**STEP
    bias_two = 1.0 - BETA_SECOND**STEP
    weight_f = weight.astype(F32)
    update = (
        new_first / bias_one / (jnp.sqrt(new_second / bias_two) + ADAM_EPS) + decay_rate * weight_f
    )
    return (gradient, weight_f - LEARN_RATE * update, new_first, new_second)


def after(value, *others):
    return lax.optimization_barrier((value, *others))[0]


class Line:
    def __init__(self):
        self.last = None

    def __call__(self, value):
        return value if self.last is None else after(value, self.last)

    def add(self, result):
        self.last = result
        return result


def chain_gather(pieces, count):
    me = lax.axis_index("dp")
    gathered = []
    gate = None
    for piece in pieces:
        up = down = piece if gate is None else after(piece, *gate)
        ups, downs = [], []
        for hop in range(1, count):
            up = lax.ppermute(up, "dp", [(k, k + 1) for k in range(hop - 1, count - 1)])
            down = lax.ppermute(down, "dp", [(k, k - 1) for k in range(1, count - hop + 1)])
            ups.append(up)
            downs.append(down)
        gate = (ups[max(count - 3, 0)], downs[max(count - 3, 0)])
        gathered.append(
            [jnp.where(me >= h, ups[h - 1], downs[count - h - 1]) for h in range(1, count)]
        )
    return gathered


def plane_scatter(total):
    size, me = lax.axis_size("tensor"), lax.axis_index("tensor")
    bits = size.bit_length() - 1
    rows = total.shape[0] // size
    own = [(me >> bit) & 1 for bit in range(bits)]

    def step(part, left, bit):
        axis = left.index(bit)
        give = lax.dynamic_index_in_dim(part, 1 - own[bit], axis, keepdims=False)
        keep = lax.dynamic_index_in_dim(part, own[bit], axis, keepdims=False)
        got = lax.ppermute(give, "tensor", [(k, k ^ (1 << bit)) for k in range(size)])
        return keep.astype(F32) + got.astype(F32), [other for other in left if other != bit]

    left = list(range(bits))[::-1]
    part, left = step(total.reshape((2,) * bits + (rows, D)), left, 0)
    halves = []
    for at, order in enumerate((list(range(1, bits)), list(range(1, bits))[::-1])):
        half = part[..., at * (D // 2) : (at + 1) * (D // 2)]
        still = left
        for bit in order:
            half, still = step(half.astype(BF16), still, bit)
        halves.append(half)
    return jnp.concatenate(halves, axis=-1)


LANES = 128
SUBLANES = 8


def all_sum_kernel(group, x_ref, out_ref, inbox, send_one, recv_one, send_two, recv_two):
    total = group[0] * group[1]
    me = lax.axis_index("dp") * group[1] + lax.axis_index("tensor")

    def place(index):
        return {"dp": index // group[1], "tensor": index % group[1]}

    def slice_of(index):
        return pl.ds(pl.multiple_of(index * SUBLANES, SUBLANES), SUBLANES)

    def spread(step):
        peer = (me + step) % total
        return pltpu.make_async_remote_copy(
            src_ref=x_ref.at[slice_of(peer)],
            dst_ref=inbox.at[me],
            send_sem=send_one.at[step],
            recv_sem=recv_one.at[me],
            device_id=place(peer),
            device_id_type=pl.DeviceIdType.MESH,
        )

    def arrive(step):
        peer = (me + step) % total
        return pltpu.make_async_remote_copy(
            src_ref=x_ref.at[slice_of(peer)],
            dst_ref=inbox.at[peer],
            send_sem=send_one.at[step],
            recv_sem=recv_one.at[peer],
            device_id=place(peer),
            device_id_type=pl.DeviceIdType.MESH,
        )

    def hand(step):
        peer = (me + step) % total
        return pltpu.make_async_remote_copy(
            src_ref=out_ref.at[slice_of(me)],
            dst_ref=out_ref.at[slice_of(me)],
            send_sem=send_two.at[step],
            recv_sem=recv_two.at[me],
            device_id=place(peer),
            device_id_type=pl.DeviceIdType.MESH,
        )

    def take(step):
        peer = (me + step) % total
        return pltpu.make_async_remote_copy(
            src_ref=out_ref.at[slice_of(me)],
            dst_ref=out_ref.at[slice_of(peer)],
            send_sem=send_two.at[step],
            recv_sem=recv_two.at[peer],
            device_id=place(peer),
            device_id_type=pl.DeviceIdType.MESH,
        )

    barrier = pltpu.get_barrier_semaphore()

    @pl.loop(1, total)
    def _(step):
        pl.semaphore_signal(
            barrier, inc=1, device_id=place((me + step) % total),
            device_id_type=pl.DeviceIdType.MESH,
        )

    pl.semaphore_wait(barrier, total - 1)

    @pl.loop(1, total)
    def _(step):
        spread(step).start()

    @pl.loop(1, total)
    def _(step):
        arrive(step).wait_recv()

    def add(step, held):
        return held + inbox[(me + step) % total]

    out_ref[slice_of(me), :] = lax.fori_loop(1, total, add, x_ref[slice_of(me), :])

    @pl.loop(1, total)
    def _(step):
        spread(step).wait_send()

    @pl.loop(1, total)
    def _(step):
        hand(step).start()

    @pl.loop(1, total)
    def _(step):
        take(step).wait_recv()

    @pl.loop(1, total)
    def _(step):
        hand(step).wait_send()


def all_sum(values):
    group = (lax.axis_size("dp"), lax.axis_size("tensor"))
    total = group[0] * group[1]
    room = total * SUBLANES * LANES
    flat = jnp.pad(values.reshape(-1), (0, room - values.size)).reshape(-1, LANES)
    summed = pl.pallas_call(
        functools.partial(all_sum_kernel, group),
        out_shape=jax.ShapeDtypeStruct(flat.shape, F32),
        in_specs=[pl.BlockSpec(memory_space=pltpu.VMEM)],
        out_specs=pl.BlockSpec(memory_space=pltpu.VMEM),
        scratch_shapes=[pltpu.VMEM((total, SUBLANES, LANES), F32)]
        + [pltpu.SemaphoreType.DMA((total,))] * 4,
        compiler_params=pltpu.CompilerParams(collective_id=0, has_side_effects=True),
        name="all_sum",
    )(flat)
    return summed.reshape(-1)[: values.size].reshape(values.shape)


def assemble(own, others, axis):
    me = lax.axis_index("dp")
    count = len(others) + 1
    width = own.shape[axis]
    shape = list(own.shape)
    shape[axis] = width * count
    full = jnp.zeros(shape, own.dtype)
    for h, shard in enumerate([own, *others]):
        full = lax.dynamic_update_slice_in_dim(full, shard, ((me - h) % count) * width, axis)
    return full


def shards(
    residual, cotangent, segments,
    in_proj, qv_bias, out_proj, up_proj, up_bias, down_proj, norm_params, out_biases,
    first_in_proj, first_qv_bias, first_out_proj, first_up_proj, first_up_bias, first_down_proj,
    first_norm_params, first_out_biases,
    second_in_proj, second_qv_bias, second_out_proj, second_up_proj, second_up_bias,
    second_down_proj, second_norm_params, second_out_biases,
):
    count = lax.axis_size("dp")
    norm_f = norm_params.astype(F32)
    width = D // count
    heads = in_proj.shape[1]
    hidden = up_proj.shape[1]
    chunk = hidden // 2

    normed, inv_std = normalize(residual)

    in_own = in_proj.reshape(width, heads * 3 * HD)
    up_size, qv_size = up_bias.shape[0], qv_bias.size
    spare = width - up_size - qv_size

    def owner_rows(biases, projections):
        rows = jnp.concatenate([biases, projections], axis=1)
        return jnp.pad(rows, ((0, 0), (0, spare)))

    bias_row = owner_rows(up_bias[None], qv_bias.reshape(1, qv_size))
    bias_rows = jnp.pad(bias_row[:, :chunk], ((0, PACK - 1), (0, max(chunk - width, 0))))
    first_piece = jnp.concatenate([up_proj[:, :chunk], bias_rows], axis=0)
    pieces = [
        first_piece, down_proj[:chunk], up_proj[:, chunk:], down_proj[chunk:], in_own, out_proj
    ]
    others = chain_gather(pieces, count)

    group_rows = lax.all_gather(residual, "tensor", axis=0, tiled=True)
    grad_rows = lax.all_gather(cotangent, "tensor", axis=0, tiled=True)
    group_f, _ = normalize(group_rows)
    mlp_rows = (group_f * norm_f[2] + norm_f[3]).astype(BF16)
    attn_rows = (group_f * norm_f[0] + norm_f[1]).astype(BF16)
    rows_all = attn_rows.shape[0]
    tables = rotation_tables(positions_of(segments).reshape(rows_all))

    line = Line()

    def scatter(total, axis):
        return lax.psum_scatter(total, "dp", scatter_dimension=axis, tiled=True).astype(F32)

    def grow(full_up, bias):
        up_rows = jnp.dot(line(mlp_rows), full_up, preferred_element_type=F32) + bias
        normal = 0.5 * (1.0 + lax.erf(up_rows * (1.0 / math.sqrt(2.0))))
        slope = normal + up_rows * jnp.exp(-0.5 * up_rows * up_rows) * (
            1.0 / math.sqrt(2.0 * math.pi)
        )
        activated = (up_rows * normal).astype(BF16)
        line.add(activated)
        return activated, slope

    def grow_back(full_down, slope):
        grad_up = dot_nt(line(grad_rows), full_down) * slope
        grad_up_r, grad_bias = grad_up.astype(BF16), jnp.sum(grad_up, axis=0)
        line.add(grad_up_r)
        return grad_up_r, grad_bias

    def weight_grad(left_op, right_op):
        return line.add(dot_tn(line(left_op), right_op).astype(BF16))

    def product(dot, left_op, right_op, *added):
        result = dot(line(left_op), right_op)
        for more in added:
            result = result + more
        return line.add(result)

    def dot_nn(left_op, right_op):
        return jnp.dot(left_op, right_op, preferred_element_type=F32)

    shard_first = [piece[:width] for piece in others[0]]
    up_a = assemble(pieces[0][:width], shard_first, 0)
    packed = assemble(
        pieces[0][width : width + 1], [piece[width : width + 1] for piece in others[0]], 0
    )
    full_upb = packed[:, :up_size].reshape(count * up_size).astype(F32)
    full_qv = (
        packed[:, up_size : up_size + qv_size]
        .reshape(count, heads, -1)
        .transpose(1, 0, 2)
        .reshape(heads, 2 * HD)
        .astype(F32)
    )
    act_a, slope_a = grow(up_a, full_upb[:chunk])
    sdown_a = scatter(weight_grad(act_a, grad_rows), 1)
    down_a = assemble(pieces[1], others[1], 1)
    gup_a, gupb_a = grow_back(down_a, slope_a)
    sup_a = scatter(weight_grad(mlp_rows, gup_a), 0)
    grad_mlp_a = product(dot_nt, gup_a, up_a)

    up_b = assemble(pieces[2], others[2], 0)
    act_b, slope_b = grow(up_b, full_upb[chunk:])
    sdown_b = scatter(weight_grad(act_b, grad_rows), 1)
    down_b = assemble(pieces[3], others[3], 1)
    gup_b, gupb_b = grow_back(down_b, slope_b)
    sup_b = scatter(weight_grad(mlp_rows, gup_b), 0)
    grad_mlp_in = product(dot_nt, gup_b, up_b, grad_mlp_a)
    branch_mlp = product(dot_nn, act_a, down_a, dot_nn(act_b, down_b))

    full_in = assemble(pieces[4], others[4], 0)
    projected = product(dot_nn, attn_rows, full_in)
    full_out = assemble(pieces[5], others[5], 1)
    grad_flat = line.add(dot_nt(line(grad_rows), full_out).astype(BF16))
    flat_out, grad_projected, grad_qv = attention(
        projected, full_qv, tables, segments, grad_flat
    )
    line.add(grad_projected)
    grad_qv = jnp.sum(grad_qv, axis=0)[:, 0, :]
    shard_in = scatter(weight_grad(attn_rows, grad_projected), 0).reshape(width, heads, 3 * HD)

    grad_rows_of = owner_rows(
        jnp.concatenate([gupb_a, gupb_b]).reshape(count, up_size),
        grad_qv.reshape(heads, count, -1).transpose(1, 0, 2).reshape(count, qv_size),
    ).reshape(1, D)
    extra = jnp.pad(grad_rows_of.astype(BF16), ((0, PACK - 1), (0, 0)))
    grad_outw = jnp.concatenate([weight_grad(flat_out, grad_rows), extra], axis=0)
    shard_last = scatter(grad_outw, 1)
    shard_outw = shard_last[: grad_outw.shape[0] - PACK]
    shard_biases = shard_last[grad_outw.shape[0] - PACK]
    shard_upb = shard_biases[:up_size]
    shard_qv = shard_biases[up_size : up_size + qv_size].reshape(qv_bias.shape)

    branch = line.add((dot_nn(line(flat_out), full_out) + branch_mlp).astype(BF16))
    local_branch = plane_scatter(branch)
    grad_attn_in = dot_nt(line(grad_projected), full_in)
    group_grad = line.add((grad_attn_in * norm_f[0] + grad_mlp_in * norm_f[2]).astype(BF16))
    grad_norms_local = jnp.stack(
        [
            jnp.sum(grad_attn_in * group_f, axis=0),
            jnp.sum(grad_attn_in, axis=0),
            jnp.sum(grad_mlp_in * group_f, axis=0),
            jnp.sum(grad_mlp_in, axis=0),
        ]
    )
    grad_normed = plane_scatter(group_grad)
    bias_out = out_biases.astype(F32)
    output = residual + local_branch + bias_out[0] + bias_out[1]

    cotangent_f = cotangent.astype(F32)
    column_sum = jnp.sum(cotangent_f, axis=0)
    sums = all_sum(jnp.concatenate([grad_norms_local, column_sum[None]], axis=0))
    grad_norms, grad_ob = sums[:4], jnp.stack([sums[4], sums[4]])
    grad_residual = cotangent_f + inv_std * (
        grad_normed
        - jnp.mean(grad_normed, axis=-1, keepdims=True)
        - normed * jnp.mean(grad_normed * normed, axis=-1, keepdims=True)
    )
    shard_upw = jnp.concatenate([sup_a, sup_b], axis=1)
    shard_down = jnp.concatenate([sdown_a, sdown_b], axis=0)

    return (
        output,
        grad_residual,
        *adamw(in_proj, shard_in, first_in_proj, second_in_proj, WEIGHT_DECAY),
        *adamw(qv_bias, shard_qv, first_qv_bias, second_qv_bias, 0.0),
        *adamw(out_proj, shard_outw, first_out_proj, second_out_proj, WEIGHT_DECAY),
        *adamw(up_proj, shard_upw, first_up_proj, second_up_proj, WEIGHT_DECAY),
        *adamw(up_bias, shard_upb, first_up_bias, second_up_bias, 0.0),
        *adamw(down_proj, shard_down, first_down_proj, second_down_proj, WEIGHT_DECAY),
        *adamw(norm_params, grad_norms, first_norm_params, second_norm_params, 0.0),
        *adamw(out_biases, grad_ob, first_out_biases, second_out_biases, 0.0),
    )


def solution(mesh):
    rows, both = P(("dp", "tensor"), None), P(("tensor", "dp"))
    heads, in_rows, in_cols = P("dp", "tensor", None), P("dp", "tensor"), P("tensor", "dp")
    params = (heads, in_cols, in_cols, in_rows, both, in_cols, P(), P())
    in_specs = (rows, rows, P("dp", None)) + params * 3
    out_specs = (rows, rows) + tuple(spec for spec in params for _ in range(4))

    return jax.shard_map(shards, mesh=mesh, in_specs=in_specs, out_specs=out_specs, check_vma=False)
```

time: 3550 us -> 2310 us (0.65)
  waiting for transfers between devices: 2360 us -> 1340 us
  local copies, waits for them, and re-layouts: 338 us -> 91.5 us
  matrix products: 574 us -> 474 us
  starting transfers between devices: 0.56 us -> 89.2 us
  blocking collectives: 81.4 us -> 0 us
  Pallas kernels: 0 us -> 71.8 us
  other arithmetic: 161 us -> 218 us
    reduce_scatter x6, waiting for transfers between devices: 1860 us -> 568 us  [scatter(): lax.psum_scatter(total, 'dp', scatter_dimension=axis, tiled=True)]
    ppermute x0 -> x46, waiting for transfers between devices: none -> 771 us  [the longest x18 670 us: chain_gather(): lax.ppermute(down, 'dp', [(k, k - 1) for k in range(1, count - hop + 1)])]
    all_gather x4 -> x0, waiting for transfers between devices: 259 us -> none  [the longest x1 182 us: shards(): lax.all_gather(in_proj, 'dp', axis=0, tiled=True)]
    all_gather x1, waiting for transfers between devices: 147 us -> 0.01 us  [shards(): group_rows = lax.all_gather(residual, 'tensor', axis=0, tiled=True)]
    dynamic_update_slice x8 -> x11, local copies, waits for them, and re-layouts: 155 us -> 14.3 us  [assemble(): lax.dynamic_update_slice_in_dim(full, shard, (me - h) % count * width, axis)]
    dot_general x18 -> x6, matrix products: 279 us -> 166 us  [the longest x4 118 us: dot_nn(): return jnp.dot(left_op, right_op, preferred_element_type=F32)]
    all_gather x1, waiting for transfers between devices: 90.1 us -> 0.01 us  [shards(): grad_rows = lax.all_gather(cotangent, 'tensor', axis=0, tiled=True)]
    ppermute x0 -> x46, starting transfers between devices: none -> 88.9 us  [the longest x18 55.1 us: chain_gather(): up = lax.ppermute(up, 'dp', [(k, k + 1) for k in range(hop - 1, count - 1)])]
  transfers between devices with their start and end apart: 14 -> 54, of which waited for: 11 -> 26; matrix products, arithmetic and copies ran while one was open for 29% -> 16% of each run, Pallas kernels for 0% -> 1%
where the time goes in v1:
time: 2310 us; the launch traced here: 2300 us
  waiting for transfers between devices  1340 us (58%)
  matrix products  474 us (21%)
  other arithmetic  218 us (9%)
  local copies, waits for them, and re-layouts  91.5 us (4%)
  starting transfers between devices  89.2 us (4%)
  Pallas kernels  71.8 us (3%)
    ppermute x18, waiting for transfers between devices, chain_gather(): lax.ppermute(down, 'dp', [(k, k - 1) for k in range(1, count - hop + 1)])  670 us
    reduce_scatter x6, waiting for transfers between devices, scatter(): lax.psum_scatter(total, 'dp', scatter_dimension=axis, tiled=True)  568 us
    dot_general x6, matrix products, dot_nt(): lax.dot_general(left_op, right_op, (((1,), (1,)), ((), ())), preferred_el...  170 us
    dot_general x6, matrix products, dot_tn(): lax.dot_general(left_op, right_op, (((0,), (0,)), ((), ())), preferred_el...  138 us
    dot_general x4, matrix products, dot_nn(): return jnp.dot(left_op, right_op, preferred_element_type=F32)  118 us
    ppermute x10, waiting for transfers between devices, step(): got = lax.ppermute(give, 'tensor', [(k, k ^ 1 << bit) for k in range(size)])  101 us
    sub x8, other arithmetic, adamw(): return (gradient, weight_f - LEARN_RATE * update, new_first, new_second)  67.8 us
    ppermute x18, starting transfers between devices, chain_gather(): up = lax.ppermute(up, 'dp', [(k, k + 1) for k in range(hop - 1, count - 1)])  55.1 us
  transfers between devices with their start and end apart: 54, of which 26 were waited for; matrix products, arithmetic and copies ran while one was open for 16% of the time, Pallas kernels for 1%

profile of v1, /device:TPU:0, one launch (start us, length us, event | category | flops | bytes accessed | tf_op | source)
XLA Modules:
  0.0 2302.6 jit_solution(12612492978327213000)
XLA Ops:
  20.1 44.0 %collective-permute-done.1 = bf16[1040,1024]{1,0:T(8,128)(2,1)S(1)} collective-permute-done((bf16[1040,1024]{1,0:T(8,128)(2,1)S(1)}, bf16[1040,1024]{1,0:T(8,128)(2,1)S(1)}, u32[]{:S(2)}, u32[]{:S(2)}) %collective-permute-start.1) | collective-permute-done | bytes 2129952 | tf_op jit(solution)/shard_map/ppermute | solution.py:201
  74.6 39.1 %collective-permute-done.2 = bf16[1040,1024]{1,0:T(8,128)(2,1)} collective-permute-done((bf16[1040,1024]{1,0:T(8,128)(2,1)S(1)}, bf16[1040,1024]{1,0:T(8,128)(2,1)}, u32[]{:S(2)}, u32[]{:S(2)}) %collective-permute-start.2) | collective-permute-done | bytes 2129952 | tf_op jit(solution)/shard_map/ppermute | solution.py:201
  121.6 41.7 %collective-permute-done.7 = bf16[1024,1024]{1,0:T(8,128)(2,1)S(1)} collective-permute-done((bf16[1024,1024]{1,0:T(8,128)(2,1)S(1)}, bf16[1024,1024]{1,0:T(8,128)(2,1)S(1)}, u32[]{:S(2)}, u32[]{:S(2)}) %collective-permute-start.7) | collective-permute-done | bytes 2097184 | tf_op jit(solution)/shard_map/ppermute | solution.py:201
  167.9 44.5 %collective-permute-done.8 = bf16[1024,1024]{1,0:T(8,128)(2,1)} collective-permute-done((bf16[1024,1024]{1,0:T(8,128)(2,1)S(1)}, bf16[1024,1024]{1,0:T(8,128)(2,1)}, u32[]{:S(2)}, u32[]{:S(2)}) %collective-permute-start.8) | collective-permute-done | bytes 2097184 | tf_op jit(solution)/shard_map/ppermute | solution.py:201
  221.7 39.0 %collective-permute-done.13 = bf16[1024,1024]{1,0:T(8,128)(2,1)} collective-permute-done((bf16[1024,1024]{1,0:T(8,128)(2,1)S(1)}, bf16[1024,1024]{1,0:T(8,128)(2,1)}, u32[]{:S(2)}, u32[]{:S(2)}) %collective-permute-start.13) | collective-permute-done | bytes 2097184 | tf_op jit(solution)/shard_map/ppermute | solution.py:201
  264.0 43.0 %collective-permute-done.14 = bf16[1024,1024]{1,0:T(8,128)(2,1)} collective-permute-done((bf16[1024,1024]{1,0:T(8,128)(2,1)}, bf16[1024,1024]{1,0:T(8,128)(2,1)}, u32[]{:S(2)}, u32[]{:S(2)}) %collective-permute-start.14) | collective-permute-done | bytes 2097184 | tf_op jit(solution)/shard_map/ppermute | solution.py:201
  315.3 39.2 %collective-permute-done.19 = bf16[1024,1024]{1,0:T(8,128)(2,1)S(1)} collective-permute-done((bf16[1024,1024]{1,0:T(8,128)(2,1)}, bf16[1024,1024]{1,0:T(8,128)(2,1)S(1)}, u32[]{:S(2)}, u32[]{:S(2)}) %collective-permute-start.19) | collective-permute-done | bytes 2097184 | tf_op jit(solution)/shard_map/ppermute | solution.py:201
  359.2 40.1 %collective-permute-done.20 = bf16[1024,1024]{1,0:T(8,128)(2,1)S(1)} collective-permute-done((bf16[1024,1024]{1,0:T(8,128)(2,1)S(1)}, bf16[1024,1024]{1,0:T(8,128)(2,1)S(1)}, u32[]{:S(2)}, u32[]{:S(2)}) %collective-permute-start.20) | collective-permute-done | bytes 2097184 | tf_op jit(solution)/shard_map/ppermute | solution.py:201
  431.1 42.5 %collective-permute-done.25 = bf16[1024,1536]{1,0:T(8,128)(2,1)} collective-permute-done((bf16[1024,1536]{1,0:T(8,128)(2,1)}, bf16[1024,1536]{1,0:T(8,128)(2,1)}, u32[]{:S(2)}, u32[]{:S(2)}) %collective-permute-start.25) | collective-permute-done | bytes 3145760 | tf_op jit(solution)/shard_map/ppermute | solution.py:201
  528.9 57.8 %collective-permute-done.26 = bf16[1024,1536]{1,0:T(8,128)(2,1)} collective-permute-done((bf16[1024,1536]{1,0:T(8,128)(2,1)}, bf16[1024,1536]{1,0:T(8,128)(2,1)}, u32[]{:S(2)}, u32[]{:S(2)}) %collective-permute-start.26) | collective-permute-done | bytes 3145760 | tf_op jit(solution)/shard_map/ppermute | solution.py:201
  595.0 36.6 %collective-permute-done.9 = bf16[1024,1024]{1,0:T(8,128)(2,1)} collective-permute-done((bf16[1024,1024]{1,0:T(8,128)(2,1)}, bf16[1024,1024]{1,0:T(8,128)(2,1)}, u32[]{:S(2)}, u32[]{:S(2)}) %collective-permute-start.9) | collective-permute-done | bytes 2097184 | tf_op jit(solution)/shard_map/ppermute | solution.py:201
  643.8 32.8 %collective-permute-done.15 = bf16[1024,1024]{1,0:T(8,128)(2,1)} collective-permute-done((bf16[1024,1024]{1,0:T(8,128)(2,1)}, bf16[1024,1024]{1,0:T(8,128)(2,1)}, u32[]{:S(2)}, u32[]{:S(2)}) %collective-permute-start.15) | collective-permute-done | bytes 2097184 | tf_op jit(solution)/shard_map/ppermute | solution.py:201
  680.9 62.9 %collective-permute-done.31 = bf16[512,1024]{1,0:T(8,128)(2,1)S(1)} collective-permute-done((bf16[512,1024]{1,0:T(8,128)(2,1)S(1)}, bf16[512,1024]{1,0:T(8,128)(2,1)S(1)}, u32[]{:S(2)}, u32[]{:S(2)}) %collective-permute-start.31) | collective-permute-done | bytes 1048608 | tf_op jit(solution)/shard_map/ppermute | solution.py:201
  757.8 71.3 %collective-permute-done.32 = bf16[512,1024]{1,0:T(8,128)(2,1)S(1)} collective-permute-done((bf16[512,1024]{1,0:T(8,128)(2,1)S(1)}, bf16[512,1024]{1,0:T(8,128)(2,1)S(1)}, u32[]{:S(2)}, u32[]{:S(2)}) %collective-permute-start.32) | collective-permute-done | bytes 1048608 | tf_op jit(solution)/shard_map/ppermute | solution.py:201
  889.9 27.1 %add_convert_fusion.3 = (bf16[2048,4096]{1,0:T(8,128)(2,1)}, bf16[2048,4096]{1,0:T(8,128)(2,1)}) fusion(f32[2048,4096]{1,0:T(8,128)} %all-gather.3.cloned.1.call-done, f32[4096]{0:T(1024)S(1)} %bitcast.148, f32[4096]{0:T(1024)S(1)} %bitcast.144, f32[2048]{0:T(1024)S(1)} %add_rsqrt_fusion, f32[2048]{0:T(1024)S(1)} %broadcast_multiply_fusion, ...), kind=kLoop, calls=%fused_computation.5 | loop fusion | flops 67108864 | bytes 67190784 | tf_op jit(solution)/shard_map/convert_element_type | solution.py:402
  963.4 27.2 %fusion.60 = (bf16[1024]{0:T(1024)(128)(2,1)S(1)}, bf16[2048,1024]{1,0:T(8,128)(2,1)}) fusion(f32[2048,1024]{1,0:T(8,128)} %get-tuple-element.152, f32[1024]{0:T(1024)S(1)} %bitcast.162, bf16[2048,4096]{1,0:T(8,128)(2,1)} %all-gather.5.cloned.1.call-done, bf16[1024,4096]{1,0:T(8,128)(2,1)} %select_dynamic-update-slice_fusion.9), kind=kOutput, calls=%fused_computation.190 | convolution fusion | flops 17205035008 | bytes 37754880 | tf_op jit(solution)/shard_map/dot_general | solution.py:65
  1015.2 25.5 %fusion.68 = f32[2048,4096]{1,0:T(8,128)} fusion(bf16[2048,1024]{1,0:T(8,128)(2,1)} %get-tuple-element.62, bf16[4096,1024]{1,0:T(8,128)(2,1)} %slice_dynamic-update-slice_fusion), kind=kOutput, calls=%fused_computation.198 | convolution fusion | flops 17179869184 | bytes 46137344 | tf_op jit(solution)/shard_map/dot_general | solution.py:65
  1088.0 25.4 %fusion.69 = f32[2048,4096]{1,0:T(8,128)} fusion(bf16[2048,1024]{1,0:T(8,128)(2,1)} %copy-done.68, bf16[1024,4096]{1,0:T(8,128)(2,1)} %select_dynamic-update-slice_fusion.3), kind=kOutput, calls=%fused_computation.199 | convolution fusion | flops 17179869184 | bytes 46137344 | tf_op jit(solution)/shard_map/dot_general | solution.py:437
  1113.3 26.2 %fusion.61 = (bf16[1024]{0:T(1024)(128)(2,1)S(1)}, bf16[2048,1024]{1,0:T(8,128)(2,1)}) fusion(f32[2048,1024]{1,0:T(8,128)S(1)} %copy-done.69, f32[1024]{0:T(1024)S(1)} %bitcast.160, bf16[2048,4096]{1,0:T(8,128)(2,1)} %all-gather.5.cloned.1.call-done, bf16[1024,4096]{1,0:T(8,128)(2,1)} %select_dynamic-update-slice_fusion.3), kind=kOutput, calls=%fused_computation.191 | convolution fusion | flops 17205035008 | bytes 37754880 | tf_op jit(solution)/shard_map/dot_general | solution.py:65
  1164.5 32.7 %convolution_add_fusion.1 = f32[2048,4096]{1,0:T(8,128)} fusion(f32[2048,4096]{1,0:T(8,128)} %fusion.68, bf16[2048,1024]{1,0:T(8,128)(2,1)} %get-tuple-element.69, bf16[4096,1024]{1,0:T(8,128)(2,1)} %select_dynamic-update-slice_fusion.6), kind=kOutput, calls=%fused_computation.9 | convolution fusion | flops 17188257792 | bytes 79691776 | tf_op jit(solution)/shard_map/dot_general | solution.py:65
  1197.2 35.8 %convolution_add_fusion = f32[2048,4096]{1,0:T(8,128)} fusion(f32[2048,4096]{1,0:T(8,128)} %fusion.69, bf16[2048,1024]{1,0:T(8,128)(2,1)} %get-tuple-element.70, bf16[1024,4096]{1,0:T(8,128)(2,1)} %select_dynamic-update-slice_fusion.9), kind=kOutput, calls=%fused_computation.8 | convolution fusion | flops 17188257792 | bytes 79691776 | tf_op jit(solution)/shard_map/dot_general | solution.py:437
  1233.0 34.2 %fusion.70.proj_ref = f32[2048,1536]{1,0:T(8,128)} fusion(bf16[2048,4096]{1,0:T(8,128)(2,1)} %get-tuple-element.77, bf16[4096,1536]{1,0:T(8,128)(2,1)} %select_dynamic-update-slice_fusion), kind=kOutput, calls=%fused_computation.200 | convolution fusion | flops 25769803776 | bytes 41943040 | tf_op jit(solution)/shard_map/dot_general | solution.py:437
  1282.0 40.8 %attention.1 = (bf16[2048,512]{1,0:T(8,128)(2,1)}, bf16[2048,1536]{1,0:T(8,128)(2,1)}, f32[2,4,1,256]{3,2,1,0:T(1,128)}) custom-call(f32[2048,1536]{1,0:T(8,128)} %fusion.70.proj_ref, f32[4,1,256]{2,1,0:T(1,128)} %reshape.241.bias_ref, f32[2048,128]{1,0:T(8,128)} %maximum_maximum_fusion.cos_ref, f32[2048,128]{1,0:T(8,128)} %get-tuple-element.139.right_ref, ...), custom_call_target="tpu_custom_call" | custom-call | flops 12884901888 | bytes 25165824 | tf_op jit(solution)/shard_map/attention/pallas_call | solution.py:130
  1323.6 33.6 %convolution_convert_fusion = bf16[4096,1536]{1,0:T(8,128)(2,1)} fusion(bf16[2048,4096]{1,0:T(8,128)(2,1)} %get-tuple-element.77, bf16[2048,1536]{1,0:T(8,128)(2,1)} %get-tuple-element.80), kind=kOutput, calls=%fused_computation.14 | convolution fusion | flops 25776095232 | bytes 35651584 | tf_op jit(solution)/shard_map/dot_general | solution.py:69
  1405.6 43.3 %multiply_reduce_fusion = (f32[4096]{0:T(1024)S(1)}, f32[4096]{0:T(1024)S(1)}, f32[4096]{0:T(1024)S(1)}, f32[4096]{0:T(1024)S(1)}, bf16[2048,4096]{1,0:T(8,128)(2,1)}) fusion(f32[2048,4096]{1,0:T(8,128)} %convolution_add_fusion.1, f32[2048,4096]{1,0:T(8,128)} %all-gather.3.cloned.1.call-done, f32[2048]{0:T(1024)S(1)} %copy-done.55, f32[2048]{0:T(1024)S(1)} %copy-done.45, ...), kind=kOutput, calls=%fused_computation | convolution fusion | flops 25870450688 | bytes 102875136 | tf_op jit(solution)/shard_map/dot_general | solution.py:65
  1528.1 40.0 %collective-permute-done.44 = bf16[2,256,2048]{2,1,0:T(8,128)(2,1)} collective-permute-done((bf16[2,256,2048]{2,1,0:T(8,128)(2,1)}, bf16[2,256,2048]{2,1,0:T(8,128)(2,1)}, u32[]{:S(2)}, u32[]{:S(2)}) %collective-permute-start.44) | collective-permute-done | bytes 2097184 | tf_op jit(solution)/shard_map/ppermute | solution.py:221
  1579.3 36.5 %collective-permute-done.45 = bf16[256,2048]{1,0:T(8,128)(2,1)S(1)} collective-permute-done((bf16[256,2048]{1,0:T(8,128)(2,1)S(1)}, bf16[256,2048]{1,0:T(8,128)(2,1)S(1)}, u32[]{:S(2)}, u32[]{:S(2)}) %collective-permute-start.45) | collective-permute-done | bytes 1048608 | tf_op jit(solution)/shard_map/ppermute | solution.py:221
  1627.0 31.0 %all_sum.1 = f32[256,128]{1,0:T(8,128)} custom-call(f32[256,128]{1,0:T(8,128)} %pad_bitcast_fusion.x_ref), custom_call_target="tpu_custom_call" | custom-call | tf_op jit(solution)/shard_map/all_sum/pallas_call | solution.py:340
  1661.2 98.0 %reduce-scatter.17.cloned.1.call-done = bf16[1024,1024]{1,0:T(8,128)(2,1)} async-done(((bf16[1024,4096]{1,0:T(8,128)(2,1)}), bf16[1024,1024]{1,0:T(8,128)(2,1)}) %reduce-scatter.17.cloned.1.call-update) | async-done | bytes 2097168 | tf_op jit(solution)/shard_map/reduce_scatter | solution.py:409
  1778.6 128.8 %reduce-scatter.11.cloned.1.call-done = bf16[1024,1024]{1,0:T(8,128)(2,1)} async-done(((bf16[4096,1024]{1,0:T(8,128)(2,1)}), bf16[1024,1024]{1,0:T(8,128)(2,1)}) %reduce-scatter.11.cloned.1.call-update) | async-done | bytes 2097168 | tf_op jit(solution)/shard_map/reduce_scatter | solution.py:409
  1907.4 148.2 %reduce-scatter.13.cloned.1.call-done = bf16[1024,1024]{1,0:T(8,128)(2,1)} async-done(((bf16[4096,1024]{1,0:T(8,128)(2,1)}), bf16[1024,1024]{1,0:T(8,128)(2,1)}) %reduce-scatter.13.cloned.1.call-update) | async-done | bytes 2097168 | tf_op jit(solution)/shard_map/reduce_scatter | solution.py:409
  2077.1 193.3 %reduce-scatter.7.cloned.1.call-done = bf16[1024,1536]{1,0:T(8,128)(2,1)} async-done(((bf16[4096,1536]{1,0:T(8,128)(2,1)}), bf16[1024,1536]{1,0:T(8,128)(2,1)}) %reduce-scatter.7.cloned.1.call-update) | async-done | bytes 3145744 | tf_op jit(solution)/shard_map/reduce_scatter | solution.py:409
  (405 shorter events, 624.3 us)
Async XLA Ops:
  7.2 857.3 %all-gather.3.cloned.1.call-start = ((), (), s32[]{:S(2)}) async-start(), calls=%async_computation.6 | async-start | bytes 37748736 | tf_op jit(solution)/shard_map/all_gather | solution.py:398
  7.9 932.2 %all-gather.5.cloned.1.call-start = ((), (), s32[]{:S(2)}) async-start(), calls=%async_computation.7 | async-start | bytes 18874368 | tf_op jit(solution)/shard_map/all_gather | solution.py:399
  12.5 51.7 %collective-permute-start.1 = (bf16[1040,1024]{1,0:T(8,128)(2,1)S(1)}, bf16[1040,1024]{1,0:T(8,128)(2,1)S(1)}, u32[]{:S(2)}, u32[]{:S(2)}) collective-permute-start(bf16[1040,1024]{1,0:T(8,128)(2,1)S(1)} %fusion.30), channel_id=1, source_target_pairs={{8,0},{16,8},{24,16},{9,1},{17,9},{25,17},{10,2},{18,10},{26,18},{... | collective-permute-start | bytes 6389768 | tf_op jit(solution)/shard_map/ppermute | solution.py:201
  14.0 51.6 %collective-permute-start = (bf16[1040,1024]{1,0:T(8,128)(2,1)S(1)}, bf16[1040,1024]{1,0:T(8,128)(2,1)S(1)}, u32[]{:S(2)}, u32[]{:S(2)}) collective-permute-start(bf16[1040,1024]{1,0:T(8,128)(2,1)S(1)} %fusion.30), channel_id=1, source_target_pairs={{0,8},{8,16},{16,24},{1,9},{9,17},{17,25},{2,10},{10,18},{18,26},{... | collective-permute-start | bytes 6389768 | tf_op jit(solution)/shard_map/ppermute | solution.py:200
  264.0 1229.0 %reduce-scatter.9.cloned.1.call-start = ((), (), s32[]{:S(2)}) async-start(), calls=%async_computation.9 | async-start | bytes 5406720 | tf_op jit(solution)/shard_map/reduce_scatter | solution.py:409
  399.3 74.3 %collective-permute-start.25 = (bf16[1024,1536]{1,0:T(8,128)(2,1)}, bf16[1024,1536]{1,0:T(8,128)(2,1)}, u32[]{:S(2)}, u32[]{:S(2)}) collective-permute-start(bf16[1024,1536]{1,0:T(8,128)(2,1)} %bitcast.58), channel_id=1, source_target_pairs={{8,0},{16,8},{24,16},{9,1},{17,9},{25,17},{10,2},{18,10},{26,18},{... | collective-permute-start | bytes 9437192 | tf_op jit(solution)/shard_map/ppermute | solution.py:201
  405.7 86.1 %collective-permute-start.24 = (bf16[1024,1536]{1,0:T(8,128)(2,1)}, bf16[1024,1536]{1,0:T(8,128)(2,1)}, u32[]{:S(2)}, u32[]{:S(2)}) collective-permute-start(bf16[1024,1536]{1,0:T(8,128)(2,1)} %bitcast.58), channel_id=1, source_target_pairs={{0,8},{8,16},{16,24},{1,9},{9,17},{17,25},{2,10},{10,18},{18,26},{... | collective-permute-start | bytes 9437192 | tf_op jit(solution)/shard_map/ppermute | solution.py:200
  413.2 106.1 %collective-permute-start.3 = (bf16[1040,1024]{1,0:T(8,128)(2,1)}, bf16[1040,1024]{1,0:T(8,128)(2,1)}, u32[]{:S(2)}, u32[]{:S(2)}) collective-permute-start(bf16[1040,1024]{1,0:T(8,128)(2,1)} %collective-permute-done.2), channel_id=1, source_target_pairs={{8,0},{9,1},{10,2},{11,3},{12,4},{13,5},{14,6},{15,7}} | collective-permute-start | bytes 6389768 | tf_op jit(solution)/shard_map/ppermute | solution.py:201
  423.0 101.4 %collective-permute-start.5 = (bf16[1040,1024]{1,0:T(8,128)(2,1)}, bf16[1040,1024]{1,0:T(8,128)(2,1)}, u32[]{:S(2)}, u32[]{:S(2)}) collective-permute-start(bf16[1040,1024]{1,0:T(8,128)(2,1)} %collective-permute-done.4), channel_id=1, source_target_pairs={{16,24},{17,25},{18,26},{19,27},{20,28},{21,29},{22,30},{23,31}} | collective-permute-start | bytes 6389768 | tf_op jit(solution)/shard_map/ppermute | solution.py:200
  473.6 113.1 %collective-permute-start.26 = (bf16[1024,1536]{1,0:T(8,128)(2,1)}, bf16[1024,1536]{1,0:T(8,128)(2,1)}, u32[]{:S(2)}, u32[]{:S(2)}) collective-permute-start(bf16[1024,1536]{1,0:T(8,128)(2,1)} %collective-permute-done.25), channel_id=1, source_target_pairs={{8,0},{16,8},{9,1},{17,9},{10,2},{18,10},{11,3},{19,11},{12,4},{20... | collective-permute-start | bytes 9437192 | tf_op jit(solution)/shard_map/ppermute | solution.py:201
  491.8 102.0 %collective-permute-start.28 = (bf16[1024,1536]{1,0:T(8,128)(2,1)}, bf16[1024,1536]{1,0:T(8,128)(2,1)}, u32[]{:S(2)}, u32[]{:S(2)}) collective-permute-start(bf16[1024,1536]{1,0:T(8,128)(2,1)} %collective-permute-done.24), channel_id=1, source_target_pairs={{8,16},{16,24},{9,17},{17,25},{10,18},{18,26},{11,19},{19,27},{12,... | collective-permute-start | bytes 9437192 | tf_op jit(solution)/shard_map/ppermute | solution.py:200
  521.1 110.5 %collective-permute-start.9 = (bf16[1024,1024]{1,0:T(8,128)(2,1)}, bf16[1024,1024]{1,0:T(8,128)(2,1)}, u32[]{:S(2)}, u32[]{:S(2)}) collective-permute-start(bf16[1024,1024]{1,0:T(8,128)(2,1)} %collective-permute-done.8), channel_id=1, source_target_pairs={{8,0},{9,1},{10,2},{11,3},{12,4},{13,5},{14,6},{15,7}} | collective-permute-start | bytes 6291464 | tf_op jit(solution)/shard_map/ppermute | solution.py:201
  522.4 114.6 %collective-permute-start.11 = (bf16[1024,1024]{1,0:T(8,128)(2,1)}, bf16[1024,1024]{1,0:T(8,128)(2,1)}, u32[]{:S(2)}, u32[]{:S(2)}) collective-permute-start(bf16[1024,1024]{1,0:T(8,128)(2,1)} %collective-permute-done.10), channel_id=1, source_target_pairs={{16,24},{17,25},{18,26},{19,27},{20,28},{21,29},{22,30},{23,31}} | collective-permute-start | bytes 6291464 | tf_op jit(solution)/shard_map/ppermute | solution.py:200
  526.2 150.4 %collective-permute-start.15 = (bf16[1024,1024]{1,0:T(8,128)(2,1)}, bf16[1024,1024]{1,0:T(8,128)(2,1)}, u32[]{:S(2)}, u32[]{:S(2)}) collective-permute-start(bf16[1024,1024]{1,0:T(8,128)(2,1)} %collective-permute-done.14), channel_id=1, source_target_pairs={{8,0},{9,1},{10,2},{11,3},{12,4},{13,5},{14,6},{15,7}} | collective-permute-start | bytes 6291464 | tf_op jit(solution)/shard_map/ppermute | solution.py:201
  586.7 93.0 %collective-permute-start.17 = (bf16[1024,1024]{1,0:T(8,128)(2,1)}, bf16[1024,1024]{1,0:T(8,128)(2,1)S(1)}, u32[]{:S(2)}, u32[]{:S(2)}) collective-permute-start(bf16[1024,1024]{1,0:T(8,128)(2,1)} %collective-permute-done.16), channel_id=1, source_target_pairs={{16,24},{17,25},{18,26},{19,27},{20,28},{21,29},{22,30},{23,31}} | collective-permute-start | bytes 6291464 | tf_op jit(solution)/shard_map/ppermute | solution.py:200
  593.7 236.7 %collective-permute-start.21 = (bf16[1024,1024]{1,0:T(8,128)(2,1)S(1)}, bf16[1024,1024]{1,0:T(8,128)(2,1)S(1)}, u32[]{:S(2)}, u32[]{:S(2)}) collective-permute-start(bf16[1024,1024]{1,0:T(8,128)(2,1)S(1)} %copy-done.32), channel_id=1, source_target_pairs={{8,0},{9,1},{10,2},{11,3},{12,4},{13,5},{14,6},{15,7}} | collective-permute-start | bytes 6291464 | tf_op jit(solution)/shard_map/ppermute | solution.py:201
  631.6 112.2 %collective-permute-start.31 = (bf16[512,1024]{1,0:T(8,128)(2,1)S(1)}, bf16[512,1024]{1,0:T(8,128)(2,1)S(1)}, u32[]{:S(2)}, u32[]{:S(2)}) collective-permute-start(bf16[512,1024]{1,0:T(8,128)(2,1)S(1)} %copy-done.20), channel_id=1, source_target_pairs={{8,0},{16,8},{24,16},{9,1},{17,9},{25,17},{10,2},{18,10},{26,18},{... | collective-permute-start | bytes 3145736 | tf_op jit(solution)/shard_map/ppermute | solution.py:201
  637.0 112.2 %collective-permute-start.30 = (bf16[512,1024]{1,0:T(8,128)(2,1)S(1)}, bf16[512,1024]{1,0:T(8,128)(2,1)S(1)}, u32[]{:S(2)}, u32[]{:S(2)}) collective-permute-start(bf16[512,1024]{1,0:T(8,128)(2,1)S(1)} %copy-done.20), channel_id=1, source_target_pairs={{0,8},{8,16},{16,24},{1,9},{9,17},{17,25},{2,10},{10,18},{18,26},{... | collective-permute-start | bytes 3145736 | tf_op jit(solution)/shard_map/ppermute | solution.py:200
  676.6 160.1 %collective-permute-start.23 = (bf16[1024,1024]{1,0:T(8,128)(2,1)S(1)}, bf16[1024,1024]{1,0:T(8,128)(2,1)S(1)}, u32[]{:S(2)}, u32[]{:S(2)}) collective-permute-start(bf16[1024,1024]{1,0:T(8,128)(2,1)S(1)} %copy-done.34), channel_id=1, source_target_pairs={{16,24},{17,25},{18,26},{19,27},{20,28},{21,29},{22,30},{23,31}} | collective-permute-start | bytes 6291464 | tf_op jit(solution)/shard_map/ppermute | solution.py:200
  679.7 173.4 %collective-permute-start.27 = (bf16[1024,1536]{1,0:T(8,128)(2,1)}, bf16[1024,1536]{1,0:T(8,128)(2,1)S(1)}, u32[]{:S(2)}, u32[]{:S(2)}) collective-permute-start(bf16[1024,1536]{1,0:T(8,128)(2,1)} %collective-permute-done.26), channel_id=1, source_target_pairs={{8,0},{9,1},{10,2},{11,3},{12,4},{13,5},{14,6},{15,7}} | collective-permute-start | bytes 9437192 | tf_op jit(solution)/shard_map/ppermute | solution.py:201
  743.9 85.3 %collective-permute-start.32 = (bf16[512,1024]{1,0:T(8,128)(2,1)S(1)}, bf16[512,1024]{1,0:T(8,128)(2,1)S(1)}, u32[]{:S(2)}, u32[]{:S(2)}) collective-permute-start(bf16[512,1024]{1,0:T(8,128)(2,1)S(1)} %collective-permute-done.31), channel_id=1, source_target_pairs={{8,0},{16,8},{9,1},{17,9},{10,2},{18,10},{11,3},{19,11},{12,4},{20... | collective-permute-start | bytes 3145736 | tf_op jit(solution)/shard_map/ppermute | solution.py:201
  749.2 84.4 %collective-permute-start.34 = (bf16[512,1024]{1,0:T(8,128)(2,1)S(1)}, bf16[512,1024]{1,0:T(8,128)(2,1)S(1)}, u32[]{:S(2)}, u32[]{:S(2)}) collective-permute-start(bf16[512,1024]{1,0:T(8,128)(2,1)S(1)} %collective-permute-done.30), channel_id=1, source_target_pairs={{8,16},{16,24},{9,17},{17,25},{10,18},{18,26},{11,19},{19,27},{12,... | collective-permute-start | bytes 3145736 | tf_op jit(solution)/shard_map/ppermute | solution.py:200
  1372.3 288.9 %reduce-scatter.15.cloned.1.call-start = ((), (), s32[]{:S(2)}) async-start(), calls=%async_computation.12 | async-start | bytes 10485760 | tf_op jit(solution)/shard_map/reduce_scatter | solution.py:409
  1372.9 386.4 %reduce-scatter.17.cloned.1.call-start = ((), (), s32[]{:S(2)}) async-start(), calls=%async_computation.13 | async-start | bytes 10485760 | tf_op jit(solution)/shard_map/reduce_scatter | solution.py:409
  1373.5 533.9 %reduce-scatter.11.cloned.1.call-start = ((), (), s32[]{:S(2)}) async-start(), calls=%async_computation.10 | async-start | bytes 10485760 | tf_op jit(solution)/shard_map/reduce_scatter | solution.py:409
  1374.0 681.5 %reduce-scatter.13.cloned.1.call-start = ((), (), s32[]{:S(2)}) async-start(), calls=%async_computation.11 | async-start | bytes 10485760 | tf_op jit(solution)/shard_map/reduce_scatter | solution.py:409
  1374.8 895.7 %reduce-scatter.7.cloned.1.call-start = ((), (), s32[]{:S(2)}) async-start(), calls=%async_computation.8 | async-start | bytes 15728640 | tf_op jit(solution)/shard_map/reduce_scatter | solution.py:409
  1405.5 57.1 %collective-permute-start.36 = (bf16[2,2,256,4096]{3,2,1,0:T(8,128)(2,1)}, bf16[2,2,256,4096]{3,2,1,0:T(8,128)(2,1)}, u32[]{:S(2)}, u32[]{:S(2)}) collective-permute-start(bf16[2,2,256,4096]{3,2,1,0:T(8,128)(2,1)} %dynamic-slice_bitcast_fusion.1), channel_id=1, source_target_pairs={{0,1},{1,0},{2,3},{3,2},{4,5},{5,4},{6,7},{7,6},{8,9},{9,8},{10,11... | collective-permute-start | bytes 25165832 | tf_op jit(solution)/shard_map/ppermute | solution.py:221
  1478.4 97.8 %collective-permute-start.37 = (bf16[2,256,2048]{2,1,0:T(8,128)(2,1)}, bf16[2,256,2048]{2,1,0:T(8,128)(2,1)}, u32[]{:S(2)}, u32[]{:S(2)}) collective-permute-start(bf16[2,256,2048]{2,1,0:T(8,128)(2,1)} %dynamic-slice_bitcast_fusion.5), channel_id=1, source_target_pairs={{0,2},{1,3},{2,0},{3,1},{4,6},{5,7},{6,4},{7,5},{8,10},{9,11},{10,... | collective-permute-start | bytes 6291464 | tf_op jit(solution)/shard_map/ppermute | solution.py:221
  1488.9 79.2 %collective-permute-start.44 = (bf16[2,256,2048]{2,1,0:T(8,128)(2,1)}, bf16[2,256,2048]{2,1,0:T(8,128)(2,1)}, u32[]{:S(2)}, u32[]{:S(2)}) collective-permute-start(bf16[2,256,2048]{2,1,0:T(8,128)(2,1)} %dynamic-slice_bitcast_fusion.2), channel_id=1, source_target_pairs={{0,4},{1,5},{2,6},{3,7},{4,0},{5,1},{6,2},{7,3},{8,12},{9,13},{10,... | collective-permute-start | bytes 6291464 | tf_op jit(solution)/shard_map/ppermute | solution.py:221
  1492.5 79.7 %collective-permute-start.42 = (bf16[2,256,2048]{2,1,0:T(8,128)(2,1)}, bf16[2,256,2048]{2,1,0:T(8,128)(2,1)}, u32[]{:S(2)}, u32[]{:S(2)}) collective-permute-start(bf16[2,256,2048]{2,1,0:T(8,128)(2,1)} %dynamic-slice_bitcast_fusion.3), channel_id=1, source_target_pairs={{0,2},{1,3},{2,0},{3,1},{4,6},{5,7},{6,4},{7,5},{8,10},{9,11},{10,... | collective-permute-start | bytes 6291464 | tf_op jit(solution)/shard_map/ppermute | solution.py:221
  1526.5 90.8 %collective-permute-start.40 = (bf16[256,2048]{1,0:T(8,128)(2,1)S(1)}, bf16[256,2048]{1,0:T(8,128)(2,1)S(1)}, u32[]{:S(2)}, u32[]{:S(2)}) collective-permute-start(bf16[256,2048]{1,0:T(8,128)(2,1)S(1)} %dynamic-slice_bitcast_fusion.8), channel_id=1, source_target_pairs={{0,2},{1,3},{2,0},{3,1},{4,6},{5,7},{6,4},{7,5},{8,10},{9,11},{10,... | collective-permute-start | bytes 3145736 | tf_op jit(solution)/shard_map/ppermute | solution.py:221
  (104 other events, 4739.2 us)
Sparse Core Ops, SparseCore 0:
  9.9 163.3 all-gather.2
  264.1 95.1 all-gather.4
  1372.4 86.7 reduce-scatter.8
  1462.0 145.1 reduce-scatter.14
  1609.9 149.3 reduce-scatter.16
  1762.1 145.2 reduce-scatter.10
  1910.3 145.2 reduce-scatter.12
  2057.9 212.4 reduce-scatter.6

commit v2 on v1

--- a/solution.py
+++ b/solution.py
@@ -6,6 +6,7 @@
 from jax import lax
 from jax.experimental import pallas as pl
 from jax.experimental.pallas import tpu as pltpu
+from jax.experimental.layout import Layout, with_layout_constraint
 from jax.sharding import PartitionSpec as P
 
 
@@ -25,6 +26,9 @@
 NEG_LARGE = -1e30
 Q_BLOCK = 256
 PACK = 16
+GROUPS = 2
+DP, TENSOR = "dp", "tensor"
+
 
 F32 = jnp.float32
 BF16 = jnp.bfloat16
@@ -173,6 +177,10 @@
     return (gradient, weight_f - LEARN_RATE * update, new_first, new_second)
 
 
+def by_rows(value):
+    return with_layout_constraint(value, Layout(major_to_minor=(0, 1)))
+
+
 def after(value, *others):
     return lax.optimization_barrier((value, *others))[0]
 
@@ -190,47 +198,56 @@
 
 
 def chain_gather(pieces, count):
-    me = lax.axis_index("dp")
+    me = lax.axis_index(DP)
     gathered = []
     gate = None
     for piece in pieces:
         up = down = piece if gate is None else after(piece, *gate)
         ups, downs = [], []
-        for hop in range(1, count):
-            up = lax.ppermute(up, "dp", [(k, k + 1) for k in range(hop - 1, count - 1)])
-            down = lax.ppermute(down, "dp", [(k, k - 1) for k in range(1, count - hop + 1)])
+        for hop in range(1, count - 1):
+            up = lax.ppermute(up, DP, [(k, k + 1) for k in range(hop - 1, count - 1)])
+            down = lax.ppermute(down, DP, [(k, k - 1) for k in range(1, count - hop + 1)])
             ups.append(up)
             downs.append(down)
         gate = (ups[max(count - 3, 0)], downs[max(count - 3, 0)])
-        gathered.append(
-            [jnp.where(me >= h, ups[h - 1], downs[count - h - 1]) for h in range(1, count)]
-        )
+        inner = lax.optimization_barrier(jnp.where(2 * me >= count, up, down))
+        ends = lax.ppermute(inner, DP, [(count - 2, count - 1), (1, 0)])
+        ups.append(ends)
+        downs.append(ends)
+        choices = [(ups[h - 1], downs[count - h - 1]) for h in range(1, count)]
+        if count == 4:
+            choices[1] = (inner, inner)
+        gathered.append(choices)
     return gathered
 
 
-def plane_scatter(total):
-    size, me = lax.axis_size("tensor"), lax.axis_index("tensor")
-    bits = size.bit_length() - 1
-    rows = total.shape[0] // size
-    own = [(me >> bit) & 1 for bit in range(bits)]
-
-    def step(part, left, bit):
-        axis = left.index(bit)
-        give = lax.dynamic_index_in_dim(part, 1 - own[bit], axis, keepdims=False)
-        keep = lax.dynamic_index_in_dim(part, own[bit], axis, keepdims=False)
-        got = lax.ppermute(give, "tensor", [(k, k ^ (1 << bit)) for k in range(size)])
-        return keep.astype(F32) + got.astype(F32), [other for other in left if other != bit]
-
-    left = list(range(bits))[::-1]
-    part, left = step(total.reshape((2,) * bits + (rows, D)), left, 0)
-    halves = []
-    for at, order in enumerate((list(range(1, bits)), list(range(1, bits))[::-1])):
-        half = part[..., at * (D // 2) : (at + 1) * (D // 2)]
-        still = left
-        for bit in order:
-            half, still = step(half.astype(BF16), still, bit)
-        halves.append(half)
-    return jnp.concatenate(halves, axis=-1)
+def chosen(choices, wait):
+    me = lax.axis_index(DP)
+    return [
+        wait(up) if up is down else jnp.where(me >= h, wait(up), wait(down))
+        for h, (up, down) in enumerate(choices, 1)
+    ]
+
+
+def chain_scatter(block_of, count):
+    me = lax.axis_index(DP)
+    first = lax.ppermute(
+        block_of(jnp.where(2 * me < count, count - 1, 0)),
+        DP,
+        [(0, 1), (count - 1, count - 2)],
+    )
+    held = (first, first)
+    for hop in range(2, count):
+        pairs = [(k, k + 1) for k in range(hop)]
+        mirrored = [(count - 1 - here, count - 1 - there) for here, there in pairs]
+        sent = []
+        for owner, partial in zip((me + count - hop, me - count + hop), held):
+            block = block_of(jnp.clip(owner, 0, count - 1))
+            sent.append((block.astype(F32) + partial.astype(F32)).astype(BF16))
+        held = lax.optimization_barrier(
+            (lax.ppermute(sent[0], DP, pairs), lax.ppermute(sent[1], DP, mirrored))
+        )
+    return block_of(me).astype(F32) + held[0].astype(F32) + held[1].astype(F32)
 
 
 LANES = 128
@@ -239,10 +256,10 @@
 
 def all_sum_kernel(group, x_ref, out_ref, inbox, send_one, recv_one, send_two, recv_two):
     total = group[0] * group[1]
-    me = lax.axis_index("dp") * group[1] + lax.axis_index("tensor")
+    me = lax.axis_index(DP) * group[1] + lax.axis_index(TENSOR)
 
     def place(index):
-        return {"dp": index // group[1], "tensor": index % group[1]}
+        return {DP: index // group[1], TENSOR: index % group[1]}
 
     def slice_of(index):
         return pl.ds(pl.multiple_of(index * SUBLANES, SUBLANES), SUBLANES)
@@ -333,7 +350,7 @@
 
 
 def all_sum(values):
-    group = (lax.axis_size("dp"), lax.axis_size("tensor"))
+    group = (lax.axis_size(DP), lax.axis_size(TENSOR))
     total = group[0] * group[1]
     room = total * SUBLANES * LANES
     flat = jnp.pad(values.reshape(-1), (0, room - values.size)).reshape(-1, LANES)
@@ -345,13 +362,12 @@
         scratch_shapes=[pltpu.VMEM((total, SUBLANES, LANES), F32)]
         + [pltpu.SemaphoreType.DMA((total,))] * 4,
         compiler_params=pltpu.CompilerParams(collective_id=0, has_side_effects=True),
-        name="all_sum",
     )(flat)
     return summed.reshape(-1)[: values.size].reshape(values.shape)
 
 
 def assemble(own, others, axis):
-    me = lax.axis_index("dp")
+    me = lax.axis_index(DP)
     count = len(others) + 1
     width = own.shape[axis]
     shape = list(own.shape)
@@ -370,7 +386,7 @@
     second_in_proj, second_qv_bias, second_out_proj, second_up_proj, second_up_bias,
     second_down_proj, second_norm_params, second_out_biases,
 ):
-    count = lax.axis_size("dp")
+    count = lax.axis_size(DP)
     norm_f = norm_params.astype(F32)
     width = D // count
     heads = in_proj.shape[1]
@@ -390,13 +406,27 @@
     bias_row = owner_rows(up_bias[None], qv_bias.reshape(1, qv_size))
     bias_rows = jnp.pad(bias_row[:, :chunk], ((0, PACK - 1), (0, max(chunk - width, 0))))
     first_piece = jnp.concatenate([up_proj[:, :chunk], bias_rows], axis=0)
+    part = heads * 3 * HD // GROUPS
+    tile = heads * HD // GROUPS
+
+    def pack(in_part, out_part):
+        stacked = [out_part[:, at : at + tile] for at in range(0, width, tile)]
+        return jnp.concatenate([in_part, jnp.concatenate(stacked, axis=0)], axis=1)
+
+    def unpack(packed):
+        rows = [packed[at : at + tile, part:] for at in range(0, width, tile)]
+        return packed[:width, :part], jnp.concatenate(rows, axis=1)
+
+    in_parts = [in_own[:, at * part : (at + 1) * part] for at in range(GROUPS)]
+    out_parts = [out_proj[at * tile : (at + 1) * tile] for at in range(GROUPS)]
     pieces = [
-        first_piece, down_proj[:chunk], up_proj[:, chunk:], down_proj[chunk:], in_own, out_proj
+        first_piece, down_proj[:chunk], up_proj[:, chunk:], down_proj[chunk:],
+        *(pack(*parts) for parts in zip(in_parts, out_parts)),
     ]
     others = chain_gather(pieces, count)
 
-    group_rows = lax.all_gather(residual, "tensor", axis=0, tiled=True)
-    grad_rows = lax.all_gather(cotangent, "tensor", axis=0, tiled=True)
+    group_rows = lax.all_gather(residual, TENSOR, axis=0, tiled=True)
+    grad_rows = lax.all_gather(cotangent, TENSOR, axis=0, tiled=True)
     group_f, _ = normalize(group_rows)
     mlp_rows = (group_f * norm_f[2] + norm_f[3]).astype(BF16)
     attn_rows = (group_f * norm_f[0] + norm_f[1]).astype(BF16)
@@ -404,9 +434,16 @@
     tables = rotation_tables(positions_of(segments).reshape(rows_all))
 
     line = Line()
+    line.add(mlp_rows)
 
     def scatter(total, axis):
-        return lax.psum_scatter(total, "dp", scatter_dimension=axis, tiled=True).astype(F32)
+        def block_of(owner):
+            return lax.dynamic_slice_in_dim(total, owner * width, width, axis)
+
+        return chain_scatter(block_of, count)
+
+    def plane_scatter(total):
+        return lax.psum_scatter(total, TENSOR, scatter_dimension=0, tiled=True).astype(F32)
 
     def grow(full_up, bias):
         up_rows = jnp.dot(line(mlp_rows), full_up, preferred_element_type=F32) + bias
@@ -428,18 +465,16 @@
         return line.add(dot_tn(line(left_op), right_op).astype(BF16))
 
     def product(dot, left_op, right_op, *added):
-        result = dot(line(left_op), right_op)
-        for more in added:
-            result = result + more
-        return line.add(result)
+        return line.add(sum(added, dot(line(left_op), right_op)))
 
     def dot_nn(left_op, right_op):
         return jnp.dot(left_op, right_op, preferred_element_type=F32)
 
-    shard_first = [piece[:width] for piece in others[0]]
+    first_others = chosen(others[0], line)
+    shard_first = [piece[:width] for piece in first_others]
     up_a = assemble(pieces[0][:width], shard_first, 0)
     packed = assemble(
-        pieces[0][width : width + 1], [piece[width : width + 1] for piece in others[0]], 0
+        pieces[0][width : width + 1], [piece[width : width + 1] for piece in first_others], 0
     )
     full_upb = packed[:, :up_size].reshape(count * up_size).astype(F32)
     full_qv = (
@@ -451,46 +486,77 @@
     )
     act_a, slope_a = grow(up_a, full_upb[:chunk])
     sdown_a = scatter(weight_grad(act_a, grad_rows), 1)
-    down_a = assemble(pieces[1], others[1], 1)
+    down_a = assemble(pieces[1], chosen(others[1], line), 1)
     gup_a, gupb_a = grow_back(down_a, slope_a)
     sup_a = scatter(weight_grad(mlp_rows, gup_a), 0)
-    grad_mlp_a = product(dot_nt, gup_a, up_a)
-
-    up_b = assemble(pieces[2], others[2], 0)
+    mlp_in_a = product(dot_nt, gup_a, up_a)
+
+    up_b = assemble(pieces[2], chosen(others[2], line), 0)
     act_b, slope_b = grow(up_b, full_upb[chunk:])
     sdown_b = scatter(weight_grad(act_b, grad_rows), 1)
-    down_b = assemble(pieces[3], others[3], 1)
+    branch_a = product(dot_nn, act_a, down_a)
+    down_b = assemble(pieces[3], chosen(others[3], line), 1)
     gup_b, gupb_b = grow_back(down_b, slope_b)
     sup_b = scatter(weight_grad(mlp_rows, gup_b), 0)
-    grad_mlp_in = product(dot_nt, gup_b, up_b, grad_mlp_a)
-    branch_mlp = product(dot_nn, act_a, down_a, dot_nn(act_b, down_b))
-
-    full_in = assemble(pieces[4], others[4], 0)
-    projected = product(dot_nn, attn_rows, full_in)
-    full_out = assemble(pieces[5], others[5], 1)
-    grad_flat = line.add(dot_nt(line(grad_rows), full_out).astype(BF16))
-    flat_out, grad_projected, grad_qv = attention(
-        projected, full_qv, tables, segments, grad_flat
-    )
-    line.add(grad_projected)
-    grad_qv = jnp.sum(grad_qv, axis=0)[:, 0, :]
-    shard_in = scatter(weight_grad(attn_rows, grad_projected), 0).reshape(width, heads, 3 * HD)
-
-    grad_rows_of = owner_rows(
-        jnp.concatenate([gupb_a, gupb_b]).reshape(count, up_size),
-        grad_qv.reshape(heads, count, -1).transpose(1, 0, 2).reshape(count, qv_size),
-    ).reshape(1, D)
-    extra = jnp.pad(grad_rows_of.astype(BF16), ((0, PACK - 1), (0, 0)))
-    grad_outw = jnp.concatenate([weight_grad(flat_out, grad_rows), extra], axis=0)
-    shard_last = scatter(grad_outw, 1)
-    shard_outw = shard_last[: grad_outw.shape[0] - PACK]
-    shard_biases = shard_last[grad_outw.shape[0] - PACK]
-    shard_upb = shard_biases[:up_size]
-    shard_qv = shard_biases[up_size : up_size + qv_size].reshape(qv_bias.shape)
-
-    branch = line.add((dot_nn(line(flat_out), full_out) + branch_mlp).astype(BF16))
-    local_branch = plane_scatter(branch)
-    grad_attn_in = dot_nt(line(grad_projected), full_in)
+    grad_mlp_in = product(dot_nt, gup_b, up_b, mlp_in_a)
+    branch_mlp = product(dot_nn, act_b, down_b, branch_a)
+
+    group = heads // GROUPS
+    full_ins, full_outs, flat_outs, grad_projs, grad_qvs, shard_groups = [], [], [], [], [], []
+    for at in range(GROUPS):
+        received = [unpack(piece) for piece in chosen(others[4 + at], line)]
+        full_in = assemble(in_parts[at], [piece[0] for piece in received], 0)
+        full_out = assemble(out_parts[at], [piece[1] for piece in received], 1)
+        projected = product(dot_nn, attn_rows, full_in)
+        grad_flat = line.add(dot_nt(line(grad_rows), full_out).astype(BF16))
+        flat_out, grad_projected, grad_qv = attention(
+            projected, full_qv[at * group : (at + 1) * group], tables, segments, grad_flat
+        )
+        line.add(grad_projected)
+        full_ins.append(full_in)
+        full_outs.append(full_out)
+        flat_outs.append(flat_out)
+        grad_projs.append(grad_projected)
+        grad_qvs.append(jnp.sum(grad_qv, axis=0)[:, 0, :])
+        final = at == GROUPS - 1
+        if final:
+            mixed = dot_nn(
+                line(jnp.concatenate(flat_outs, axis=1)), jnp.concatenate(full_outs, axis=0)
+            )
+            branch = line.add((mixed + branch_mlp).astype(BF16))
+            local_branch = plane_scatter(branch)
+            bias_rows_of = owner_rows(
+                jnp.concatenate([gupb_a, gupb_b]).reshape(count, up_size),
+                jnp.concatenate(grad_qvs, axis=0)
+                .reshape(heads, count, -1)
+                .transpose(1, 0, 2)
+                .reshape(count, qv_size),
+            ).astype(BF16)
+        grad_inw = weight_grad(attn_rows, grad_projected)
+        grad_outw = weight_grad(flat_out, grad_rows)
+
+        def owner_block(owner, grad_inw=grad_inw, grad_outw=grad_outw, final=final):
+            block = pack(
+                lax.dynamic_slice_in_dim(grad_inw, owner * width, width, 0),
+                lax.dynamic_slice_in_dim(grad_outw, owner * width, width, 1),
+            )
+            if not final:
+                return block
+            row = lax.dynamic_slice_in_dim(bias_rows_of, owner, 1, 0)
+            return jnp.concatenate([block, jnp.pad(row, ((0, PACK - 1), (0, 0)))], axis=0)
+
+        shard_groups.append(chain_scatter(owner_block, count))
+    unpacked = [unpack(shard) for shard in shard_groups]
+    shard_in = jnp.concatenate(
+        [shard.reshape(width, group, 3 * HD) for shard, _ in unpacked], axis=1
+    )
+    shard_outw = by_rows(jnp.concatenate([shard for _, shard in unpacked], axis=0))
+    shard_upb = shard_groups[-1][width, :up_size]
+    shard_qv = shard_groups[-1][width, up_size : up_size + qv_size].reshape(qv_bias.shape)
+
+    grad_attn_in = dot_nt(
+        line(jnp.concatenate(grad_projs, axis=1)), jnp.concatenate(full_ins, axis=1)
+    )
     group_grad = line.add((grad_attn_in * norm_f[0] + grad_mlp_in * norm_f[2]).astype(BF16))
     grad_norms_local = jnp.stack(
         [
@@ -504,37 +570,44 @@
     bias_out = out_biases.astype(F32)
     output = residual + local_branch + bias_out[0] + bias_out[1]
 
-    cotangent_f = cotangent.astype(F32)
-    column_sum = jnp.sum(cotangent_f, axis=0)
-    sums = all_sum(jnp.concatenate([grad_norms_local, column_sum[None]], axis=0))
+    column_sum = jnp.sum(cotangent.astype(F32), axis=0)
+    cotangent_f = after(cotangent, column_sum).astype(F32)
+    local_sums = jnp.concatenate([grad_norms_local, column_sum[None]], axis=0)
+    sums = all_sum(after(local_sums, shard_upb))
     grad_norms, grad_ob = sums[:4], jnp.stack([sums[4], sums[4]])
     grad_residual = cotangent_f + inv_std * (
         grad_normed
         - jnp.mean(grad_normed, axis=-1, keepdims=True)
         - normed * jnp.mean(grad_normed * normed, axis=-1, keepdims=True)
     )
-    shard_upw = jnp.concatenate([sup_a, sup_b], axis=1)
+    shard_upw = jnp.concatenate([by_rows(sup_a), by_rows(sup_b)], axis=1)
     shard_down = jnp.concatenate([sdown_a, sdown_b], axis=0)
+    result_in = adamw(in_proj, shard_in, first_in_proj, second_in_proj, WEIGHT_DECAY)
+    result_out = adamw(out_proj, shard_outw, first_out_proj, second_out_proj, WEIGHT_DECAY)
+    result_up = adamw(up_proj, shard_upw, first_up_proj, second_up_proj, WEIGHT_DECAY)
+    result_down = adamw(
+        down_proj, shard_down, first_down_proj, second_down_proj, WEIGHT_DECAY
+    )
 
     return (
         output,
         grad_residual,
-        *adamw(in_proj, shard_in, first_in_proj, second_in_proj, WEIGHT_DECAY),
+        *result_in,
         *adamw(qv_bias, shard_qv, first_qv_bias, second_qv_bias, 0.0),
-        *adamw(out_proj, shard_outw, first_out_proj, second_out_proj, WEIGHT_DECAY),
-        *adamw(up_proj, shard_upw, first_up_proj, second_up_proj, WEIGHT_DECAY),
+        *result_out,
+        *result_up,
         *adamw(up_bias, shard_upb, first_up_bias, second_up_bias, 0.0),
-        *adamw(down_proj, shard_down, first_down_proj, second_down_proj, WEIGHT_DECAY),
+        *result_down,
         *adamw(norm_params, grad_norms, first_norm_params, second_norm_params, 0.0),
         *adamw(out_biases, grad_ob, first_out_biases, second_out_biases, 0.0),
     )
 
 
 def solution(mesh):
-    rows, both = P(("dp", "tensor"), None), P(("tensor", "dp"))
-    heads, in_rows, in_cols = P("dp", "tensor", None), P("dp", "tensor"), P("tensor", "dp")
+    rows, both = P((DP, TENSOR), None), P((TENSOR, DP))
+    heads, in_rows, in_cols = P(DP, TENSOR, None), P(DP, TENSOR), P(TENSOR, DP)
     params = (heads, in_cols, in_cols, in_rows, both, in_cols, P(), P())
-    in_specs = (rows, rows, P("dp", None)) + params * 3
+    in_specs = (rows, rows, P(DP, None)) + params * 3
     out_specs = (rows, rows) + tuple(spec for spec in params for _ in range(4))
 
     return jax.shard_map(shards, mesh=mesh, in_specs=in_specs, out_specs=out_specs, check_vma=False)

time: 2310 us -> 2230 us (0.965)
  waiting for transfers between devices: 1340 us -> 1010 us
  other arithmetic: 218 us -> 333 us
  starting transfers between devices: 89.2 us -> 163 us
  local copies, waits for them, and re-layouts: 91.5 us -> 134 us
  matrix products: 474 us -> 499 us
    reduce_scatter x6 -> x2, waiting for transfers between devices: 568 us -> 0.04 us  [plane_scatter(): lax.psum_scatter(total, TENSOR, scatter_dimension=0, tiled=True).astype(F32)]
    ppermute x46 -> x60, waiting for transfers between devices: 771 us -> 1010 us  [the longest x12 336 us: chain_scatter(): lax.ppermute(sent[0], DP, pairs)]
    convert_element_type x5 -> x14, other arithmetic: 11 us -> 89.7 us  [chain_scatter(): sent.append((block.astype(F32) + partial.astype(F32)).astype(BF16))]
    ppermute x46 -> x60, starting transfers between devices: 88.9 us -> 163 us  [the longest x12 67.9 us: chain_scatter(): lax.ppermute(sent[0], DP, pairs)]
    add x2 -> x6, other arithmetic: 0.72 us -> 35.3 us  [chain_scatter(): return block_of(me).astype(F32) + held[0].astype(F32) + held[1].astype(F32)]
    dynamic_update_slice x15 -> x12, other arithmetic: 44.3 us -> 18.7 us  [assemble(): lax.dynamic_update_slice_in_dim(full, shard, (me - h) % count * width, axis)]
    dot_general x6 -> x8, matrix products: 138 us -> 156 us  [dot_tn(): lax.dot_general(left_op, right_op, (((0,), (0,)), ((), ())), preferred_el...]
    dot_general x4 -> x5, matrix products: 118 us -> 122 us  [dot_nn(): return jnp.dot(left_op, right_op, preferred_element_type=F32)]
  transfers between devices with their start and end apart: 54 -> 64, of which waited for: 26 -> 33; matrix products, arithmetic and copies ran while one was open for 16% -> 36% of each run, Pallas kernels for 1% -> 2%
where the time goes in v2:
time: 2230 us; the launch traced here: 2220 us
  waiting for transfers between devices  1010 us (45%)
  matrix products  499 us (22%)
  other arithmetic  333 us (15%)
  starting transfers between devices  163 us (7%)
  local copies, waits for them, and re-layouts  134 us (6%)
  Pallas kernels  62.2 us (3%)
    ppermute x12, waiting for transfers between devices, chain_scatter(): lax.ppermute(sent[0], DP, pairs)  336 us
    ppermute x12, waiting for transfers between devices, chain_gather(): lax.ppermute(down, DP, [(k, k - 1) for k in range(1, count - hop + 1)])  256 us
    ppermute x12, waiting for transfers between devices, chain_gather(): up = lax.ppermute(up, DP, [(k, k + 1) for k in range(hop - 1, count - 1)])  219 us
    ppermute x6, waiting for transfers between devices, chain_scatter(): lax.ppermute(block_of(jnp.where(2 * me < count, count - 1, 0)), DP, [(0,...  202 us
    dot_general x7, matrix products, dot_nt(): lax.dot_general(left_op, right_op, (((1,), (1,)), ((), ())), preferred_el...  172 us
    dot_general x8, matrix products, dot_tn(): lax.dot_general(left_op, right_op, (((0,), (0,)), ((), ())), preferred_el...  156 us
    dot_general x5, matrix products, dot_nn(): return jnp.dot(left_op, right_op, preferred_element_type=F32)  122 us
    convert_element_type x14, other arithmetic, chain_scatter(): sent.append((block.astype(F32) + partial.astype(F32)).astype(BF16))  89.7 us
  transfers between devices with their start and end apart: 64, of which 33 were waited for; matrix products, arithmetic and copies ran while one was open for 36% of the time, Pallas kernels for 2%

profile of v2, /device:TPU:0, one launch (start us, length us, event | category | flops | bytes accessed | tf_op | source)
XLA Modules:
  0.0 2221.4 jit_solution(16820870318753491413)
XLA Ops:
  25.4 43.9 %collective-permute-done = bf16[1040,1024]{1,0:T(8,128)(2,1)S(1)} collective-permute-done((bf16[1040,1024]{1,0:T(8,128)(2,1)S(1)}, bf16[1040,1024]{1,0:T(8,128)(2,1)S(1)}, u32[]{:S(2)}, u32[]{:S(2)}) %collective-permute-start) | collective-permute-done | bytes 2129952 | tf_op jit(solution)/shard_map/ppermute | solution.py:208
  83.2 40.5 %collective-permute-done.3 = bf16[1040,1024]{1,0:T(8,128)(2,1)} collective-permute-done((bf16[1040,1024]{1,0:T(8,128)(2,1)S(1)}, bf16[1040,1024]{1,0:T(8,128)(2,1)}, u32[]{:S(2)}, u32[]{:S(2)}) %collective-permute-start.3) | collective-permute-done | bytes 2129952 | tf_op jit(solution)/shard_map/ppermute | solution.py:209
  128.7 41.3 %collective-permute-done.5 = bf16[1024,1024]{1,0:T(8,128)(2,1)S(1)} collective-permute-done((bf16[1024,1024]{1,0:T(8,128)(2,1)S(1)}, bf16[1024,1024]{1,0:T(8,128)(2,1)S(1)}, u32[]{:S(2)}, u32[]{:S(2)}) %collective-permute-start.5) | collective-permute-done | bytes 2097184 | tf_op jit(solution)/shard_map/ppermute | solution.py:208
  176.9 45.2 %collective-permute-done.8 = bf16[1024,1024]{1,0:T(8,128)(2,1)} collective-permute-done((bf16[1024,1024]{1,0:T(8,128)(2,1)S(1)}, bf16[1024,1024]{1,0:T(8,128)(2,1)}, u32[]{:S(2)}, u32[]{:S(2)}) %collective-permute-start.8) | collective-permute-done | bytes 2097184 | tf_op jit(solution)/shard_map/ppermute | solution.py:209
  228.4 38.7 %collective-permute-done.10 = bf16[1024,1024]{1,0:T(8,128)(2,1)} collective-permute-done((bf16[1024,1024]{1,0:T(8,128)(2,1)}, bf16[1024,1024]{1,0:T(8,128)(2,1)}, u32[]{:S(2)}, u32[]{:S(2)}) %collective-permute-start.10) | collective-permute-done | bytes 2097184 | tf_op jit(solution)/shard_map/ppermute | solution.py:208
  274.2 43.3 %collective-permute-done.13 = bf16[1024,1024]{1,0:T(8,128)(2,1)S(1)} collective-permute-done((bf16[1024,1024]{1,0:T(8,128)(2,1)}, bf16[1024,1024]{1,0:T(8,128)(2,1)S(1)}, u32[]{:S(2)}, u32[]{:S(2)}) %collective-permute-start.13) | collective-permute-done | bytes 2097184 | tf_op jit(solution)/shard_map/ppermute | solution.py:209
  320.4 38.1 %collective-permute-done.15 = bf16[1024,1024]{1,0:T(8,128)(2,1)S(1)} collective-permute-done((bf16[1024,1024]{1,0:T(8,128)(2,1)}, bf16[1024,1024]{1,0:T(8,128)(2,1)S(1)}, u32[]{:S(2)}, u32[]{:S(2)}) %collective-permute-start.15) | collective-permute-done | bytes 2097184 | tf_op jit(solution)/shard_map/ppermute | solution.py:208
  375.6 33.5 %collective-permute-done.18 = bf16[1024,1024]{1,0:T(8,128)(2,1)S(1)} collective-permute-done((bf16[1024,1024]{1,0:T(8,128)(2,1)S(1)}, bf16[1024,1024]{1,0:T(8,128)(2,1)S(1)}, u32[]{:S(2)}, u32[]{:S(2)}) %collective-permute-start.18) | collective-permute-done | bytes 2097184 | tf_op jit(solution)/shard_map/ppermute | solution.py:209
  412.4 34.5 %collective-permute-done.20 = bf16[1024,1024]{1,0:T(8,128)(2,1)S(1)} collective-permute-done((bf16[1024,1024]{1,0:T(8,128)(2,1)S(1)}, bf16[1024,1024]{1,0:T(8,128)(2,1)S(1)}, u32[]{:S(2)}, u32[]{:S(2)}) %collective-permute-start.20) | collective-permute-done | bytes 2097184 | tf_op jit(solution)/shard_map/ppermute | solution.py:208
  566.5 33.7 %collective-permute-done.28 = bf16[1024,1024]{1,0:T(8,128)(2,1)S(1)} collective-permute-done((bf16[1024,1024]{1,0:T(8,128)(2,1)}, bf16[1024,1024]{1,0:T(8,128)(2,1)S(1)}, u32[]{:S(2)}, u32[]{:S(2)}) %collective-permute-start.28) | collective-permute-done | bytes 2097184 | tf_op jit(solution)/shard_map/ppermute | solution.py:209
  628.2 26.9 %add_convert_fusion.3 = (bf16[2048,4096]{1,0:T(8,128)(2,1)}, bf16[2048,4096]{1,0:T(8,128)(2,1)}) fusion(f32[2048,4096]{1,0:T(8,128)} %all-gather.3.cloned.1.call-done, f32[4096]{0:T(1024)S(1)} %bitcast.105, f32[4096]{0:T(1024)S(1)} %bitcast.101, f32[2048]{0:T(1024)S(1)} %add_rsqrt_fusion, f32[2048]{0:T(1024)S(1)} %broadcast_multiply_fusion, ...), kind=kLoop, calls=%fused_computation.5 | loop fusion | flops 67108864 | bytes 67190784 | tf_op jit(solution)/shard_map/convert_element_type | solution.py:432
  667.5 25.0 %multiply_convert_fusion.1 = (bf16[2048,1024]{1,0:T(8,128)(2,1)}, f32[2048,1024]{1,0:T(8,128)}) fusion(f32[1024]{0:T(1024)S(1)} %bitcast.117, bf16[2048,4096]{1,0:T(8,128)(2,1)} %get-tuple-element.145, bf16[4096,1024]{1,0:T(8,128)(2,1)} %slice_dynamic-update-slice_fusion), kind=kOutput, calls=%fused_computation.45 | convolution fusion | flops 17192452096 | bytes 37752832 | tf_op jit(solution)/shard_map/dot_general | solution.py:449
  725.3 27.9 %fusion.84 = (bf16[1024]{0:T(1024)(128)(2,1)}, bf16[2048,1024]{1,0:T(8,128)(2,1)}) fusion(f32[2048,1024]{1,0:T(8,128)} %get-tuple-element.401, f32[1024]{0:T(1024)S(1)} %bitcast.118, bf16[2048,4096]{1,0:T(8,128)(2,1)} %all-gather.5.cloned.1.call-done, bf16[1024,4096]{1,0:T(8,128)(2,1)} %select_dynamic-update-slice_fusion.4), kind=kOutput, calls=%fused_computation.321 | convolution fusion | flops 17205035008 | bytes 37754880 | tf_op jit(solution)/shard_map/dot_general | solution.py:69
  753.2 25.4 %convolution_convert_fusion.2 = bf16[4096,1024]{1,0:T(8,128)(2,1)} fusion(bf16[2048,4096]{1,0:T(8,128)(2,1)} %get-tuple-element.145, bf16[2048,1024]{1,0:T(8,128)(2,1)} %get-tuple-element.130), kind=kOutput, calls=%fused_computation.51 | convolution fusion | flops 17184063488 | bytes 29360128 | tf_op jit(solution)/shard_map/dot_general | solution.py:73
  811.8 24.8 %multiply_convert_fusion = (bf16[2048,1024]{1,0:T(8,128)(2,1)S(1)}, f32[2048,1024]{1,0:T(8,128)}) fusion(f32[1024]{0:T(1024)S(1)} %bitcast.115, bf16[2048,4096]{1,0:T(8,128)(2,1)} %get-tuple-element.145, bf16[4096,1024]{1,0:T(8,128)(2,1)} %select_dynamic-update-slice_fusion.2), kind=kOutput, calls=%fused_computation.43 | convolution fusion | flops 17192452096 | bytes 37752832 | tf_op jit(solution)/shard_map/dot_general | solution.py:449
  858.9 23.6 %fusion.102 = f32[2048,4096]{1,0:T(8,128)} fusion(bf16[2048,1024]{1,0:T(8,128)(2,1)S(1)} %copy-done.119, bf16[1024,4096]{1,0:T(8,128)(2,1)} %select_dynamic-update-slice_fusion.4), kind=kOutput, calls=%fused_computation.339 | convolution fusion | flops 17179869184 | bytes 46137344 | tf_op jit(solution)/shard_map/dot_general | solution.py:471
  888.6 27.0 %fusion.85 = (bf16[1024]{0:T(1024)(128)(2,1)}, bf16[2048,1024]{1,0:T(8,128)(2,1)S(1)}) fusion(f32[2048,1024]{1,0:T(8,128)} %get-tuple-element.404, f32[1024]{0:T(1024)S(1)} %bitcast.116, bf16[2048,4096]{1,0:T(8,128)(2,1)} %all-gather.5.cloned.1.call-done, bf16[1024,4096]{1,0:T(8,128)(2,1)S(1)} %select_dynamic-update-slice_fusion), kind=kOutput, calls=%fused_computation.322 | convolution fusion | flops 17205035008 | bytes 37754880 | tf_op jit(solution)/shard_map/dot_general | solution.py:69
  940.6 32.8 %convolution_add_fusion.1 = f32[2048,4096]{1,0:T(8,128)} fusion(f32[2048,4096]{1,0:T(8,128)} %fusion.101, bf16[2048,1024]{1,0:T(8,128)(2,1)} %copy-done.121, bf16[4096,1024]{1,0:T(8,128)(2,1)} %select_dynamic-update-slice_fusion.2), kind=kOutput, calls=%fused_computation.9 | convolution fusion | flops 17188257792 | bytes 79691776 | tf_op jit(solution)/shard_map/dot_general | solution.py:69
  973.3 35.8 %convolution_add_fusion = f32[2048,4096]{1,0:T(8,128)} fusion(f32[2048,4096]{1,0:T(8,128)} %fusion.102, bf16[2048,1024]{1,0:T(8,128)(2,1)} %copy-done.120, bf16[1024,4096]{1,0:T(8,128)(2,1)} %copy-done.19), kind=kOutput, calls=%fused_computation.8 | convolution fusion | flops 17188257792 | bytes 79691776 | tf_op jit(solution)/shard_map/dot_general | solution.py:471
  1227.5 43.1 %multiply_reduce_fusion = (f32[4096]{0:T(1024)}, f32[4096]{0:T(1024)}, f32[4096]{0:T(1024)}, f32[4096]{0:T(1024)}, bf16[2048,4096]{1,0:T(8,128)(2,1)}) fusion(f32[2048,4096]{1,0:T(8,128)} %convolution_add_fusion.1, f32[2048,4096]{1,0:T(8,128)} %all-gather.3.cloned.1.call-done, f32[2048]{0:T(1024)S(1)} %copy-done.105, f32[2048]{0:T(1024)S(1)} %copy-done.93, ...), kind=kOutput, calls=%fused_computation | convolution fusion | flops 25895616512 | bytes 102875136 | tf_op jit(solution)/shard_map/dot_general | solution.py:69
  1349.3 32.1 %collective-permute-done.45 = bf16[1024,1024]{1,0:T(8,128)(2,1)} collective-permute-done((bf16[1024,1024]{1,0:T(8,128)(2,1)}, bf16[1024,1024]{1,0:T(8,128)(2,1)}, u32[]{:S(2)}, u32[]{:S(2)}) %collective-permute-start.45) | collective-permute-done | bytes 2097184 | tf_op jit(solution)/shard_map/ppermute | solution.py:234
  1387.1 39.3 %collective-permute-done.40 = bf16[1024,1024]{1,0:T(8,128)(2,1)} collective-permute-done((bf16[1024,1024]{1,0:T(8,128)(2,1)}, bf16[1024,1024]{1,0:T(8,128)(2,1)}, u32[]{:S(2)}, u32[]{:S(2)}) %collective-permute-start.40) | collective-permute-done | bytes 2097184 | tf_op jit(solution)/shard_map/ppermute | solution.py:234
  1439.6 77.3 %collective-permute-done.55 = bf16[1024,1024]{1,0:T(8,128)(2,1)} collective-permute-done((bf16[1024,1024]{1,0:T(8,128)(2,1)}, bf16[1024,1024]{1,0:T(8,128)(2,1)}, u32[]{:S(2)}, u32[]{:S(2)}) %collective-permute-start.55) | collective-permute-done | bytes 2097184 | tf_op jit(solution)/shard_map/ppermute | solution.py:234
  1521.5 40.4 %collective-permute-done.50 = bf16[1024,1024]{1,0:T(8,128)(2,1)} collective-permute-done((bf16[1024,1024]{1,0:T(8,128)(2,1)}, bf16[1024,1024]{1,0:T(8,128)(2,1)}, u32[]{:S(2)}, u32[]{:S(2)}) %collective-permute-start.50) | collective-permute-done | bytes 2097184 | tf_op jit(solution)/shard_map/ppermute | solution.py:234
  1572.7 34.1 %collective-permute-done.31 = bf16[1024,1024]{1,0:T(8,128)(2,1)} collective-permute-done((bf16[1024,1024]{1,0:T(8,128)(2,1)}, bf16[1024,1024]{1,0:T(8,128)(2,1)}, u32[]{:S(2)}, u32[]{:S(2)}) %collective-permute-start.31) | collective-permute-done | bytes 2097184 | tf_op jit(solution)/shard_map/ppermute | solution.py:248
  1619.0 32.8 %collective-permute-done.46 = bf16[1024,1024]{1,0:T(8,128)(2,1)S(1)} collective-permute-done((bf16[1024,1024]{1,0:T(8,128)(2,1)}, bf16[1024,1024]{1,0:T(8,128)(2,1)S(1)}, u32[]{:S(2)}, u32[]{:S(2)}) %collective-permute-start.46) | collective-permute-done | bytes 2097184 | tf_op jit(solution)/shard_map/ppermute | solution.py:248
  1664.7 31.9 %collective-permute-done.41 = bf16[1024,1024]{1,0:T(8,128)(2,1)S(1)} collective-permute-done((bf16[1024,1024]{1,0:T(8,128)(2,1)S(1)}, bf16[1024,1024]{1,0:T(8,128)(2,1)S(1)}, u32[]{:S(2)}, u32[]{:S(2)}) %collective-permute-start.41) | collective-permute-done | bytes 2097184 | tf_op jit(solution)/shard_map/ppermute | solution.py:248
  1705.2 36.4 %collective-permute-done.56 = bf16[1024,1024]{1,0:T(8,128)(2,1)} collective-permute-done((bf16[1024,1024]{1,0:T(8,128)(2,1)S(1)}, bf16[1024,1024]{1,0:T(8,128)(2,1)}, u32[]{:S(2)}, u32[]{:S(2)}) %collective-permute-start.56) | collective-permute-done | bytes 2097184 | tf_op jit(solution)/shard_map/ppermute | solution.py:248
  1775.7 56.5 %collective-permute-done.51 = bf16[1024,1024]{1,0:T(8,128)(2,1)} collective-permute-done((bf16[1024,1024]{1,0:T(8,128)(2,1)}, bf16[1024,1024]{1,0:T(8,128)(2,1)}, u32[]{:S(2)}, u32[]{:S(2)}) %collective-permute-start.51) | collective-permute-done | bytes 2097184 | tf_op jit(solution)/shard_map/ppermute | solution.py:248
  1884.8 37.2 %collective-permute-done.48 = bf16[1024,1024]{1,0:T(8,128)(2,1)} collective-permute-done((bf16[1024,1024]{1,0:T(8,128)(2,1)S(1)}, bf16[1024,1024]{1,0:T(8,128)(2,1)}, u32[]{:S(2)}, u32[]{:S(2)}) %collective-permute-start.48) | collective-permute-done | bytes 2097184 | tf_op jit(solution)/shard_map/ppermute | solution.py:248
  1929.8 37.2 %collective-permute-done.43 = bf16[1024,1024]{1,0:T(8,128)(2,1)} collective-permute-done((bf16[1024,1024]{1,0:T(8,128)(2,1)S(1)}, bf16[1024,1024]{1,0:T(8,128)(2,1)}, u32[]{:S(2)}, u32[]{:S(2)}) %collective-permute-start.43) | collective-permute-done | bytes 2097184 | tf_op jit(solution)/shard_map/ppermute | solution.py:248
  2013.5 38.5 %collective-permute-done.53 = bf16[1024,1024]{1,0:T(8,128)(2,1)} collective-permute-done((bf16[1024,1024]{1,0:T(8,128)(2,1)}, bf16[1024,1024]{1,0:T(8,128)(2,1)}, u32[]{:S(2)}, u32[]{:S(2)}) %collective-permute-start.53) | collective-permute-done | bytes 2097184 | tf_op jit(solution)/shard_map/ppermute | solution.py:248
  (601 shorter events, 1026.4 us)
Async XLA Ops:
  7.2 596.0 %all-gather.3.cloned.1.call-start = ((), (), s32[]{:S(2)}) async-start(), calls=%async_computation.2 | async-start | bytes 37748736 | tf_op jit(solution)/shard_map/all_gather | solution.py:428
  8.0 684.5 %all-gather.5.cloned.1.call-start = ((), (), s32[]{:S(2)}) async-start(), calls=%async_computation.3 | async-start | bytes 18874368 | tf_op jit(solution)/shard_map/all_gather | solution.py:429
  228.4 1975.3 %reduce-scatter.5.cloned.1.call-start = ((), (), s32[]{:S(2)}) async-start(), calls=%async_computation.5 | async-start | bytes 18874368 | tf_op jit(solution)/shard_map/reduce_scatter | solution.py:446
  552.7 102.4 %collective-permute-start.4 = (bf16[1040,1024]{1,0:T(8,128)(2,1)S(1)}, bf16[1040,1024]{1,0:T(8,128)(2,1)}, u32[]{:S(2)}, u32[]{:S(2)}) collective-permute-start(bf16[1040,1024]{1,0:T(8,128)(2,1)S(1)} %broadcast_select_fusion.1), channel_id=1, source_target_pairs={{16,24},{8,0},{17,25},{9,1},{18,26},{10,2},{19,27},{11,3},{20,28},... | collective-permute-start | bytes 6389768 | tf_op jit(solution)/shard_map/ppermute | solution.py:214
  557.4 158.4 %collective-permute-start.9 = (bf16[1024,1024]{1,0:T(8,128)(2,1)}, bf16[1024,1024]{1,0:T(8,128)(2,1)}, u32[]{:S(2)}, u32[]{:S(2)}) collective-permute-start(bf16[1024,1024]{1,0:T(8,128)(2,1)} %broadcast_select_fusion.9), channel_id=1, source_target_pairs={{16,24},{8,0},{17,25},{9,1},{18,26},{10,2},{19,27},{11,3},{20,28},... | collective-permute-start | bytes 6291464 | tf_op jit(solution)/shard_map/ppermute | solution.py:214
  560.5 240.2 %collective-permute-start.14 = (bf16[1024,1024]{1,0:T(8,128)(2,1)}, bf16[1024,1024]{1,0:T(8,128)(2,1)}, u32[]{:S(2)}, u32[]{:S(2)}) collective-permute-start(bf16[1024,1024]{1,0:T(8,128)(2,1)} %broadcast_select_fusion.8), channel_id=1, source_target_pairs={{16,24},{8,0},{17,25},{9,1},{18,26},{10,2},{19,27},{11,3},{20,28},... | collective-permute-start | bytes 6291464 | tf_op jit(solution)/shard_map/ppermute | solution.py:214
  565.2 317.3 %collective-permute-start.19 = (bf16[1024,1024]{1,0:T(8,128)(2,1)}, bf16[1024,1024]{1,0:T(8,128)(2,1)}, u32[]{:S(2)}, u32[]{:S(2)}) collective-permute-start(bf16[1024,1024]{1,0:T(8,128)(2,1)} %broadcast_select_fusion.7), channel_id=1, source_target_pairs={{16,24},{8,0},{17,25},{9,1},{18,26},{10,2},{19,27},{11,3},{20,28},... | collective-permute-start | bytes 6291464 | tf_op jit(solution)/shard_map/ppermute | solution.py:214
  600.2 409.7 %collective-permute-start.24 = (bf16[1024,1024]{1,0:T(8,128)(2,1)}, bf16[1024,1024]{1,0:T(8,128)(2,1)}, u32[]{:S(2)}, u32[]{:S(2)}) collective-permute-start(bf16[1024,1024]{1,0:T(8,128)(2,1)} %broadcast_select_fusion.6), channel_id=1, source_target_pairs={{16,24},{8,0},{17,25},{9,1},{18,26},{10,2},{19,27},{11,3},{20,28},... | collective-permute-start | bytes 6291464 | tf_op jit(solution)/shard_map/ppermute | solution.py:214
  655.2 447.9 %collective-permute-start.29 = (bf16[1024,1024]{1,0:T(8,128)(2,1)}, bf16[1024,1024]{1,0:T(8,128)(2,1)}, u32[]{:S(2)}, u32[]{:S(2)}) collective-permute-start(bf16[1024,1024]{1,0:T(8,128)(2,1)} %broadcast_select_fusion.5), channel_id=1, source_target_pairs={{16,24},{8,0},{17,25},{9,1},{18,26},{10,2},{19,27},{11,3},{20,28},... | collective-permute-start | bytes 6291464 | tf_op jit(solution)/shard_map/ppermute | solution.py:214
  1270.7 937.1 %reduce-scatter.3.cloned.1.call-start = ((), (), s32[]{:S(2)}) async-start(), calls=%async_computation.4 | async-start | bytes 18874368 | tf_op jit(solution)/shard_map/reduce_scatter | solution.py:446
  1301.2 125.2 %collective-permute-start.40 = (bf16[1024,1024]{1,0:T(8,128)(2,1)}, bf16[1024,1024]{1,0:T(8,128)(2,1)}, u32[]{:S(2)}, u32[]{:S(2)}) collective-permute-start(bf16[1024,1024]{1,0:T(8,128)(2,1)} %constant_dynamic-slice_fusion.38), channel_id=1, source_target_pairs={{0,8},{24,16},{1,9},{25,17},{2,10},{26,18},{3,11},{27,19},{4,12},{... | collective-permute-start | bytes 6291464 | tf_op jit(solution)/shard_map/ppermute | solution.py:234
  1312.0 255.5 %collective-permute-start.35 = (bf16[1040,1024]{1,0:T(8,128)(2,1)}, bf16[1040,1024]{1,0:T(8,128)(2,1)}, u32[]{:S(2)}, u32[]{:S(2)}) collective-permute-start(bf16[1040,1024]{1,0:T(8,128)(2,1)} %fusion.53), channel_id=1, source_target_pairs={{0,8},{24,16},{1,9},{25,17},{2,10},{26,18},{3,11},{27,19},{4,12},{... | collective-permute-start | bytes 6389768 | tf_op jit(solution)/shard_map/ppermute | solution.py:234
  1317.7 199.2 %collective-permute-start.55 = (bf16[1024,1024]{1,0:T(8,128)(2,1)}, bf16[1024,1024]{1,0:T(8,128)(2,1)}, u32[]{:S(2)}, u32[]{:S(2)}) collective-permute-start(bf16[1024,1024]{1,0:T(8,128)(2,1)} %constant_dynamic-slice_fusion.35), channel_id=1, source_target_pairs={{0,8},{24,16},{1,9},{25,17},{2,10},{26,18},{3,11},{27,19},{4,12},{... | collective-permute-start | bytes 6291464 | tf_op jit(solution)/shard_map/ppermute | solution.py:234
  1336.5 225.4 %collective-permute-start.50 = (bf16[1024,1024]{1,0:T(8,128)(2,1)}, bf16[1024,1024]{1,0:T(8,128)(2,1)}, u32[]{:S(2)}, u32[]{:S(2)}) collective-permute-start(bf16[1024,1024]{1,0:T(8,128)(2,1)} %constant_dynamic-slice_fusion.36), channel_id=1, source_target_pairs={{0,8},{24,16},{1,9},{25,17},{2,10},{26,18},{3,11},{27,19},{4,12},{... | collective-permute-start | bytes 6291464 | tf_op jit(solution)/shard_map/ppermute | solution.py:234
  1381.4 225.4 %collective-permute-start.31 = (bf16[1024,1024]{1,0:T(8,128)(2,1)}, bf16[1024,1024]{1,0:T(8,128)(2,1)}, u32[]{:S(2)}, u32[]{:S(2)}) collective-permute-start(bf16[1024,1024]{1,0:T(8,128)(2,1)} %get-tuple-element.318), channel_id=1, source_target_pairs={{0,8},{8,16},{1,9},{9,17},{2,10},{10,18},{3,11},{11,19},{4,12},{12... | collective-permute-start | bytes 6291464 | tf_op jit(solution)/shard_map/ppermute | solution.py:248
  1426.4 182.5 %collective-permute-start.32 = (bf16[1024,1024]{1,0:T(8,128)(2,1)}, bf16[1024,1024]{1,0:T(8,128)(2,1)}, u32[]{:S(2)}, u32[]{:S(2)}) collective-permute-start(bf16[1024,1024]{1,0:T(8,128)(2,1)} %get-tuple-element.317), channel_id=1, source_target_pairs={{24,16},{16,8},{25,17},{17,9},{26,18},{18,10},{27,19},{19,11},{28,... | collective-permute-start | bytes 6291464 | tf_op jit(solution)/shard_map/ppermute | solution.py:248
  1516.9 134.8 %collective-permute-start.46 = (bf16[1024,1024]{1,0:T(8,128)(2,1)}, bf16[1024,1024]{1,0:T(8,128)(2,1)S(1)}, u32[]{:S(2)}, u32[]{:S(2)}) collective-permute-start(bf16[1024,1024]{1,0:T(8,128)(2,1)} %get-tuple-element.245), channel_id=1, source_target_pairs={{0,8},{8,16},{1,9},{9,17},{2,10},{10,18},{3,11},{11,19},{4,12},{12... | collective-permute-start | bytes 6291464 | tf_op jit(solution)/shard_map/ppermute | solution.py:248
  1561.9 95.5 %collective-permute-start.47 = (bf16[1024,1024]{1,0:T(8,128)(2,1)S(1)}, bf16[1024,1024]{1,0:T(8,128)(2,1)S(1)}, u32[]{:S(2)}, u32[]{:S(2)}) collective-permute-start(bf16[1024,1024]{1,0:T(8,128)(2,1)S(1)} %get-tuple-element.244), channel_id=1, source_target_pairs={{24,16},{16,8},{25,17},{17,9},{26,18},{18,10},{27,19},{19,11},{28,... | collective-permute-start | bytes 6291464 | tf_op jit(solution)/shard_map/ppermute | solution.py:248
  1567.6 129.0 %collective-permute-start.41 = (bf16[1024,1024]{1,0:T(8,128)(2,1)S(1)}, bf16[1024,1024]{1,0:T(8,128)(2,1)S(1)}, u32[]{:S(2)}, u32[]{:S(2)}) collective-permute-start(bf16[1024,1024]{1,0:T(8,128)(2,1)S(1)} %get-tuple-element.243), channel_id=1, source_target_pairs={{0,8},{8,16},{1,9},{9,17},{2,10},{10,18},{3,11},{11,19},{4,12},{12... | collective-permute-start | bytes 6291464 | tf_op jit(solution)/shard_map/ppermute | solution.py:248
  1606.8 93.1 %collective-permute-start.42 = (bf16[1024,1024]{1,0:T(8,128)(2,1)S(1)}, bf16[1024,1024]{1,0:T(8,128)(2,1)}, u32[]{:S(2)}, u32[]{:S(2)}) collective-permute-start(bf16[1024,1024]{1,0:T(8,128)(2,1)S(1)} %get-tuple-element.242), channel_id=1, source_target_pairs={{24,16},{16,8},{25,17},{17,9},{26,18},{18,10},{27,19},{19,11},{28,... | collective-permute-start | bytes 6291464 | tf_op jit(solution)/shard_map/ppermute | solution.py:248
  1608.8 132.7 %collective-permute-start.56 = (bf16[1024,1024]{1,0:T(8,128)(2,1)S(1)}, bf16[1024,1024]{1,0:T(8,128)(2,1)}, u32[]{:S(2)}, u32[]{:S(2)}) collective-permute-start(bf16[1024,1024]{1,0:T(8,128)(2,1)S(1)} %get-tuple-element.241), channel_id=1, source_target_pairs={{0,8},{8,16},{1,9},{9,17},{2,10},{10,18},{3,11},{11,19},{4,12},{12... | collective-permute-start | bytes 6291464 | tf_op jit(solution)/shard_map/ppermute | solution.py:248
  1651.8 188.2 %collective-permute-start.36 = (bf16[1040,1024]{1,0:T(8,128)(2,1)}, bf16[1040,1024]{1,0:T(8,128)(2,1)}, u32[]{:S(2)}, u32[]{:S(2)}) collective-permute-start(bf16[1040,1024]{1,0:T(8,128)(2,1)} %get-tuple-element.290), channel_id=1, source_target_pairs={{0,8},{8,16},{1,9},{9,17},{2,10},{10,18},{3,11},{11,19},{4,12},{12... | collective-permute-start | bytes 6389768 | tf_op jit(solution)/shard_map/ppermute | solution.py:248
  1657.4 183.8 %collective-permute-start.37 = (bf16[1040,1024]{1,0:T(8,128)(2,1)}, bf16[1040,1024]{1,0:T(8,128)(2,1)}, u32[]{:S(2)}, u32[]{:S(2)}) collective-permute-start(bf16[1040,1024]{1,0:T(8,128)(2,1)} %get-tuple-element.289), channel_id=1, source_target_pairs={{24,16},{16,8},{25,17},{17,9},{26,18},{18,10},{27,19},{19,11},{28,... | collective-permute-start | bytes 6389768 | tf_op jit(solution)/shard_map/ppermute | solution.py:248
  1699.9 132.3 %collective-permute-start.51 = (bf16[1024,1024]{1,0:T(8,128)(2,1)}, bf16[1024,1024]{1,0:T(8,128)(2,1)}, u32[]{:S(2)}, u32[]{:S(2)}) collective-permute-start(bf16[1024,1024]{1,0:T(8,128)(2,1)} %get-tuple-element.239), channel_id=1, source_target_pairs={{0,8},{8,16},{1,9},{9,17},{2,10},{10,18},{3,11},{11,19},{4,12},{12... | collective-permute-start | bytes 6291464 | tf_op jit(solution)/shard_map/ppermute | solution.py:248
  1741.6 92.0 %collective-permute-start.52 = (bf16[1024,1024]{1,0:T(8,128)(2,1)}, bf16[1024,1024]{1,0:T(8,128)(2,1)}, u32[]{:S(2)}, u32[]{:S(2)}) collective-permute-start(bf16[1024,1024]{1,0:T(8,128)(2,1)} %get-tuple-element.238), channel_id=1, source_target_pairs={{24,16},{16,8},{25,17},{17,9},{26,18},{18,10},{27,19},{19,11},{28,... | collective-permute-start | bytes 6291464 | tf_op jit(solution)/shard_map/ppermute | solution.py:248
  1770.6 106.6 %collective-permute-start.33 = (bf16[1024,1024]{1,0:T(8,128)(2,1)}, bf16[1024,1024]{1,0:T(8,128)(2,1)}, u32[]{:S(2)}, u32[]{:S(2)}) collective-permute-start(bf16[1024,1024]{1,0:T(8,128)(2,1)} %add_convert_fusion.15), channel_id=1, source_target_pairs={{0,8},{8,16},{16,24},{1,9},{9,17},{17,25},{2,10},{10,18},{18,26},{... | collective-permute-start | bytes 6291464 | tf_op jit(solution)/shard_map/ppermute | solution.py:248
  1841.2 125.7 %collective-permute-start.43 = (bf16[1024,1024]{1,0:T(8,128)(2,1)S(1)}, bf16[1024,1024]{1,0:T(8,128)(2,1)}, u32[]{:S(2)}, u32[]{:S(2)}) collective-permute-start(bf16[1024,1024]{1,0:T(8,128)(2,1)S(1)} %get-tuple-element.251), channel_id=1, source_target_pairs={{0,8},{8,16},{16,24},{1,9},{9,17},{17,25},{2,10},{10,18},{18,26},{... | collective-permute-start | bytes 6291464 | tf_op jit(solution)/shard_map/ppermute | solution.py:248
  1877.2 112.4 %collective-permute-start.44 = (bf16[1024,1024]{1,0:T(8,128)(2,1)}, bf16[1024,1024]{1,0:T(8,128)(2,1)}, u32[]{:S(2)}, u32[]{:S(2)}) collective-permute-start(bf16[1024,1024]{1,0:T(8,128)(2,1)} %get-tuple-element.250), channel_id=1, source_target_pairs={{24,16},{16,8},{8,0},{25,17},{17,9},{9,1},{26,18},{18,10},{10,2},{... | collective-permute-start | bytes 6291464 | tf_op jit(solution)/shard_map/ppermute | solution.py:248
  1878.5 133.5 %collective-permute-start.58 = (bf16[1024,1024]{1,0:T(8,128)(2,1)}, bf16[1024,1024]{1,0:T(8,128)(2,1)}, u32[]{:S(2)}, u32[]{:S(2)}) collective-permute-start(bf16[1024,1024]{1,0:T(8,128)(2,1)} %get-tuple-element.249), channel_id=1, source_target_pairs={{0,8},{8,16},{16,24},{1,9},{9,17},{17,25},{2,10},{10,18},{18,26},{... | collective-permute-start | bytes 6291464 | tf_op jit(solution)/shard_map/ppermute | solution.py:248
  1923.3 128.6 %collective-permute-start.53 = (bf16[1024,1024]{1,0:T(8,128)(2,1)}, bf16[1024,1024]{1,0:T(8,128)(2,1)}, u32[]{:S(2)}, u32[]{:S(2)}) collective-permute-start(bf16[1024,1024]{1,0:T(8,128)(2,1)} %get-tuple-element.247), channel_id=1, source_target_pairs={{0,8},{8,16},{16,24},{1,9},{9,17},{17,25},{2,10},{10,18},{18,26},{... | collective-permute-start | bytes 6291464 | tf_op jit(solution)/shard_map/ppermute | solution.py:248
  1989.6 148.8 %collective-permute-start.38 = (bf16[1040,1024]{1,0:T(8,128)(2,1)}, bf16[1040,1024]{1,0:T(8,128)(2,1)}, u32[]{:S(2)}, u32[]{:S(2)}) collective-permute-start(bf16[1040,1024]{1,0:T(8,128)(2,1)} %add_convert_fusion.5), channel_id=1, source_target_pairs={{0,8},{8,16},{16,24},{1,9},{9,17},{17,25},{2,10},{10,18},{18,26},{... | collective-permute-start | bytes 6389768 | tf_op jit(solution)/shard_map/ppermute | solution.py:248
  2012.0 126.4 %collective-permute-start.39 = (bf16[1040,1024]{1,0:T(8,128)(2,1)}, bf16[1040,1024]{1,0:T(8,128)(2,1)}, u32[]{:S(2)}, u32[]{:S(2)}) collective-permute-start(bf16[1040,1024]{1,0:T(8,128)(2,1)} %add_convert_fusion.4), channel_id=1, source_target_pairs={{24,16},{16,8},{8,0},{25,17},{17,9},{9,1},{26,18},{18,10},{10,2},{... | collective-permute-start | bytes 6389768 | tf_op jit(solution)/shard_map/ppermute | solution.py:248
  (177 other events, 5702.9 us)
Sparse Core Ops, SparseCore 0:
  9.9 163.3 all-gather.2
  228.5 90.0 all-gather.4
  1270.8 116.2 reduce-scatter.4
  1428.5 117.8 reduce-scatter.2
